TPU v7x, 32 devices: a whole 2x2x4 slice. The times are simulated.
32 devices in a mesh: dp: 4 (over x, y), tp: 8 (over z, core).
Axes of the slice: x: 2, y: 2, z: 4, core: 2. Of those that a mesh axis runs over, the one named last changes fastest.
Arguments:
- hidden: bfloat16 [2048, 2048], P(('dp', 'tp')), parts along dimension 0
- cache_lat: bfloat16 [2048, 512, 512], P(('dp', 'tp')), parts along dimension 0
- cache_rope: bfloat16 [2048, 512, 64], P(('dp', 'tp')), parts along dimension 0
- seq_lens: int32 [2048], P(('dp', 'tp')), parts along dimension 0
- attn_norm: bfloat16 [2048], replicated
- w_query: bfloat16 [2048, 3072], replicated
- w_kv_down: bfloat16 [2048, 576], replicated
- kv_norm: bfloat16 [512], replicated
- w_key_up: bfloat16 [512, 2048], replicated
- w_val_up: bfloat16 [512, 2048], replicated
- w_out: bfloat16 [2048, 2048], replicated
- mlp_norm: bfloat16 [2048], replicated
- w_gate: bfloat16 [2048, 10944], P(None, 'tp')
- w_up: bfloat16 [2048, 10944], P(None, 'tp')
- w_down: bfloat16 [10944, 2048], P('tp')
Outputs:
- output 1: bfloat16 [2048, 2048], P(('dp', 'tp')), parts along dimension 0
- output 2: bfloat16 [2048, 512], P(('dp', 'tp')), parts along dimension 0
- output 3: bfloat16 [2048, 64], P(('dp', 'tp')), parts along dimension 0
There are 4 independent parts. A program takes and returns all parts, laid end to end along the dimension named above; an argument that names none is the same for every part.
All inputs are finite; a program needn't handle non-finite values.
Results may differ from a plain program's by a relative error of at most 0.0106894.
Values are sent between devices in bfloat16 or wider.
A program may use at most 1 GiB of HBM per device.

v0:
```python
import jax
import jax.numpy as jnp
from jax import lax
from jax.sharding import PartitionSpec as P

EPS = 1e-6
ROPE_BASE = 10000.0
value_a7 = 512
ROPE_DIM = 64
NOPE_DIM = 128
SCALE = (NOPE_DIM + ROPE_DIM) ** -0.5


def rms_norm(vals, gain):
    vals32 = vals.astype(jnp.float32)
    inv_rms = lax.rsqrt(jnp.mean(vals32 * vals32, axis=-1, keepdims=True) + EPS)
    return (vals32 * inv_rms * gain.astype(jnp.float32)).astype(jnp.bfloat16)


def rotate(vals, cos_tab, sin_tab):
    half = vals.shape[-1] // 2
    first = vals[..., :half]
    second = vals[..., half:]
    return jnp.concatenate([first * cos_tab - second * sin_tab, second * cos_tab + first * sin_tab], axis=-1)


def rope_tables(seq_lens):
    inv_freq = ROPE_BASE ** (-jnp.arange(0, ROPE_DIM, 2, dtype=jnp.float32) / ROPE_DIM)
    angles = seq_lens.astype(jnp.float32)[:, None] * inv_freq[None, :]
    return jnp.cos(angles), jnp.sin(angles)


def attention_block(hidden, cache_lat, cache_rope, seq_lens, attn_norm, w_query, w_kv_down, kv_norm, w_key_up, w_val_up, w_out):
    rows = hidden.shape[0]
    heads = w_key_up.shape[1] // NOPE_DIM
    normed = rms_norm(hidden, attn_norm)
    query = jnp.dot(normed, w_query, preferred_element_type=jnp.float32).astype(jnp.bfloat16).reshape(rows, heads, NOPE_DIM + ROPE_DIM)
    kv_proj = jnp.dot(normed, w_kv_down, preferred_element_type=jnp.float32).astype(jnp.bfloat16)
    lat_new = rms_norm(kv_proj[:, :value_a7], kv_norm)
    cos_tab, sin_tab = rope_tables(seq_lens)
    rope_new = rotate(kv_proj[:, value_a7:].astype(jnp.float32), cos_tab, sin_tab).astype(jnp.bfloat16)
    q_rot = rotate(query[:, :, NOPE_DIM:].astype(jnp.float32), cos_tab[:, None, :], sin_tab[:, None, :]).astype(jnp.bfloat16)
    key_up = w_key_up.reshape(value_a7, heads, NOPE_DIM)
    q_lat = jnp.einsum('bhn,khn->bhk', query[:, :, :NOPE_DIM], key_up, preferred_element_type=jnp.float32).astype(jnp.bfloat16)
    scores = (jnp.einsum('bhk,bsk->bhs', q_lat, cache_lat, preferred_element_type=jnp.float32) + jnp.einsum('bhr,bsr->bhs', q_rot, cache_rope, preferred_element_type=jnp.float32)) * SCALE
    score_new = (jnp.einsum('bhk,bk->bh', q_lat, lat_new, preferred_element_type=jnp.float32) + jnp.einsum('bhr,br->bh', q_rot, rope_new, preferred_element_type=jnp.float32)) * SCALE
    slots = cache_lat.shape[1]
    valid = jnp.arange(slots)[None, None, :] < seq_lens[:, None, None]
    scores = jnp.where(valid, scores, -jnp.inf)
    top = jnp.maximum(jnp.max(scores, axis=-1), score_new)
    expo = jnp.exp(scores - top[..., None])
    expo_new = jnp.exp(score_new - top)
    denom = jnp.sum(expo, axis=-1) + expo_new
    probs = (expo / denom[..., None]).astype(jnp.bfloat16)
    prob_new = (expo_new / denom).astype(jnp.bfloat16)
    lat_sum = jnp.einsum('bhs,bsk->bhk', probs, cache_lat, preferred_element_type=jnp.float32) + prob_new.astype(jnp.float32)[..., None] * lat_new.astype(jnp.float32)[:, None, :]
    lat_out = lat_sum.astype(jnp.bfloat16)
    val_up = w_val_up.reshape(value_a7, heads, -1)
    head_out = jnp.einsum('bhk,khv->bhv', lat_out, val_up, preferred_element_type=jnp.float32).astype(jnp.bfloat16).reshape(rows, -1)
    attn_out = jnp.dot(head_out, w_out, preferred_element_type=jnp.float32)
    resid = (hidden.astype(jnp.float32) + attn_out).astype(jnp.bfloat16)
    return resid, lat_new, rope_new


def solution(mesh):
    rows_spec = P(('dp', 'tp'), None)
    cache_spec = P(('dp', 'tp'), None, None)
    whole = P()
    in_specs = (rows_spec, cache_spec, cache_spec, P(('dp', 'tp')), whole, whole, whole, whole, whole, whole, whole, whole, P(None, 'tp'), P(None, 'tp'), P('tp', None))
    out_specs = (rows_spec, rows_spec, rows_spec)

    def device_step(hidden, cache_lat, cache_rope, seq_lens, attn_norm, w_query, w_kv_down, kv_norm, w_key_up, w_val_up, w_out, mlp_norm, w_gate, w_up, w_down):
        resid, lat_new, rope_new = attention_block(hidden, cache_lat, cache_rope, seq_lens, attn_norm, w_query, w_kv_down, kv_norm, w_key_up, w_val_up, w_out)
        mlp_in = rms_norm(resid, mlp_norm)
        group_in = lax.all_gather(mlp_in, 'tp', axis=0, tiled=True)
        gate_proj = jnp.dot(group_in, w_gate, preferred_element_type=jnp.float32)
        up_proj = jnp.dot(group_in, w_up, preferred_element_type=jnp.float32)
        act = (jax.nn.silu(gate_proj) * up_proj).astype(jnp.bfloat16)
        partial_out = jnp.dot(act, w_down, preferred_element_type=jnp.float32).astype(jnp.bfloat16)
        mlp_out = lax.psum_scatter(partial_out, 'tp', scatter_dimension=0, tiled=True)
        out_hidden = (resid.astype(jnp.float32) + mlp_out.astype(jnp.float32)).astype(jnp.bfloat16)
        return out_hidden, lat_new, rope_new

    return jax.shard_map(device_step, mesh=mesh, in_specs=in_specs, out_specs=out_specs, check_vma=False)
```

profile of v0, /device:TPU:0, one launch (start us, length us, event | category | flops | bytes accessed | tf_op | source)
XLA Modules:
  0.0 164.7 jit_solution(16066647032935045616)
XLA Ops:
  7.2 0.0 copy-start
  7.2 0.0 copy-start.2
  7.2 0.0 all-gather.2.cloned.1.call-start
  7.3 0.8 convert_element_type.95
  8.1 0.7 iota_compare_fusion
  8.8 1.1 fusion.33
  9.9 0.7 convert_element_type.89
  10.6 0.0 copy-done
  10.6 1.8 %convolution_convert_fusion.2 = bf16[64,576]{1,0:T(8,128)(2,1)S(1)} fusion(bf16[2048,576]{0,1:T(8,128)(2,1)S(1)} %copy-done, bf16[64,2048]{1,0:T(8,128)(2,1)} %param.15, f32[2048]{0:T(1024)S(1)} %convert_element_type.89, f32[64]{0:T(128)S(1)} %add_rsqrt_fusion.2), kind=kOutput, calls=%fused_computation.23 | convolution fusion | flops 151556096 | bytes 2703616 | tf_op jit(solution)/shard_map/dot_general | solution.py:38
  12.4 0.1 fusion.39
  12.5 0.0 copy-done.2
  12.5 6.9 %convolution_convert_fusion = bf16[64,3072]{1,0:T(8,128)(2,1)S(1)} fusion(bf16[2048,3072]{1,0:T(8,128)(2,1)} %param.20, bf16[64,2048]{1,0:T(8,128)(2,1)S(1)} %copy-done.2, f32[2048]{0:T(1024)S(1)} %convert_element_type.89, f32[64]{0:T(128)S(1)} %add_rsqrt_fusion.2), kind=kOutput, calls=%fused_computation | convolution fusion | flops 806027264 | bytes 13246720 | tf_op jit(solution)/shard_map/dot_general | solution.py:37
  19.5 0.0 copy-start.5
  19.5 0.0 copy-start.4
  19.5 0.6 reshape.122
  20.2 0.0 copy-done.5
  20.2 0.0 copy-done.4
  20.3 0.1 fusion.53
  20.4 0.0 copy-start.3
  20.4 2.5 %fusion.14 = bf16[64,16,512]{2,0,1:T(8,128)(2,1)S(1)} fusion(bf16[64,16,128]{2,1,0:T(8,128)(2,1)S(1)} %slice.32, bf16[512,2048]{1,0:T(8,128)(2,1)} %param.23), kind=kOutput, calls=%fused_computation.20 | convolution fusion | flops 134742016 | bytes 3407872 | tf_op jit(solution)/shard_map/bhn,khn->bhk/dot_general | solution.py:44
  22.9 0.7 fusion.29
  23.6 0.0 copy-done.3
  23.6 14.6 %fusion.31 = f32[64,16,512]{2,1,0:T(8,128)S(1)} fusion(bf16[64,512,512]{2,1,0:T(8,128)(2,1)} %param.16, bf16[64,16,512]{2,0,1:T(8,128)(2,1)S(1)} %fusion.14), kind=kOutput, calls=%fused_computation.31 | convolution fusion | flops 536870912 | bytes 36700160 | tf_op jit(solution)/shard_map/bhk,bsk->bhs/dot_general | solution.py:45
  38.2 0.2 subtract_convert_fusion.1
  38.4 0.1 fusion.68
  38.5 0.2 subtract_convert_fusion
  38.7 0.3 fusion.45
  39.1 3.2 %fusion.55 = (f32[64,16]{1,0:T(8,128)S(1)}, f32[64,16,512]{2,1,0:T(8,128)S(1)}) fusion(f32[64,16,512]{2,1,0:T(8,128)S(1)} %fusion.31, bf16[64,512,64]{1,2,0:T(8,128)(2,1)} %param.17, bf16[64,16,32]{2,1,0:T(8,128)(2,1)S(1)} %get-tuple-element.6, bf16[64,16,32]{2,1,0:T(8,128)(2,1)S(1)} %get-tuple-element.5, pred[64,512]{1,0:T(8,128)(4,1)S(1)} %iota_compare_fusion), kind=kOutput, calls=%fused_computation.77 | convolution fusion | flops 69467136 | bytes 8556544 | tf_op jit(solution)/shard_map/bhr,bsr->bhs/dot_general | solution.py:45
  42.2 0.6 fusion.10
  42.9 14.3 %fusion.23 = f32[64,16,512]{2,1,0:T(8,128)} fusion(bf16[64,512,512]{2,1,0:T(8,128)(2,1)} %param.16, f32[64,16,512]{2,1,0:T(8,128)S(1)} %get-tuple-element.14, f32[64,16]{1,0:T(8,128)S(1)} %get-tuple-element.8, f32[64,16]{1,0:T(8,128)S(1)} %fusion.48), kind=kOutput, calls=%fused_computation.24 | convolution fusion | flops 538443776 | bytes 37756928 | tf_op jit(solution)/shard_map/bhs,bsk->bhk/dot_general | solution.py:56
  57.1 0.1 copy.26
  57.2 3.8 %fusion.20 = bf16[16,8,8,128]{3,2,1,0:T(8,128)(2,1)S(1)} fusion(f32[64,16,512]{2,1,0:T(8,128)} %fusion.23, f32[64,512]{1,0:T(8,128)S(1)} %get-tuple-element.3, f32[64,16]{0,1:T(8,128)S(1)} %copy.26, bf16[512,2048]{1,0:T(8,128)(2,1)} %param.24), kind=kOutput, calls=%fused_computation.22 | convolution fusion | flops 135921664 | bytes 4591616 | tf_op jit(solution)/shard_map/bhk,khv->bhv/dot_general | solution.py:59
  61.0 5.1 %multiply_reduce_fusion = (f32[64]{0:T(128)S(1)}, f32[64,2048]{1,0:T(8,128)S(1)}) fusion(bf16[2048,2048]{1,0:T(8,128)(2,1)} %param.25, bf16[16,8,8,128]{3,2,1,0:T(8,128)(2,1)S(1)} %fusion.20, bf16[64,2048]{1,0:T(8,128)(2,1)S(1)} %copy-done.2), kind=kOutput, calls=%fused_computation.40 | convolution fusion | flops 537657280 | bytes 9437440 | tf_op jit(solution)/shard_map/dot_general | solution.py:60
  66.1 0.8 multiply_convert_fusion
  66.9 0.0 all-gather.2.cloned.1.call-update
  66.9 0.3 reduce-scatter.2.cloned.1.call-start
  67.2 31.7 %all-gather.2.cloned.1.call-done = bf16[512,2048]{1,0:T(8,128)(2,1)} async-done(((bf16[64,2048]{1,0:T(8,128)(2,1)}), bf16[512,2048]{1,0:T(8,128)(2,1)}) %all-gather.2.cloned.1.call-update) | async-done | bytes 2097168 | tf_op jit(solution)/shard_map/all_gather | solution.py:75
  98.9 7.9 %fusion.56 = f32[512,1368]{0,1:T(8,128)} fusion(bf16[512,2048]{1,0:T(8,128)(2,1)} %all-gather.2.cloned.1.call-done, bf16[2048,1368]{0,1:T(8,128)(2,1)} %param.27), kind=kOutput, calls=%fused_computation.78 | convolution fusion | flops 2868903936 | bytes 10502144 | tf_op jit(solution)/shard_map/dot_general | solution.py:76
  106.8 0.0 copy-start.1
  106.8 13.9 %convolution_convert_fusion.1 = bf16[512,2048]{1,0:T(8,128)(2,1)} fusion(bf16[1368,2048]{1,0:T(8,128)(2,1)} %param.29, bf16[512,2048]{1,0:T(8,128)(2,1)} %all-gather.2.cloned.1.call-done, bf16[2048,1368]{0,1:T(8,128)(2,1)} %param.28, f32[512,1368]{0,1:T(8,128)} %fusion.56), kind=kOutput, calls=%fused_computation.3 | convolution fusion | flops 5743058944 | bytes 18202624 | tf_op jit(solution)/shard_map/dot_general | solution.py:79
  120.7 0.0 reduce-scatter.2.cloned.1.call-update
  120.7 0.7 pad_maximum_fusion.3
  121.4 34.7 %reduce-scatter.2.cloned.1.call-done = bf16[64,2048]{1,0:T(8,128)(2,1)} async-done(((bf16[512,2048]{1,0:T(8,128)(2,1)}), bf16[64,2048]{1,0:T(8,128)(2,1)}) %reduce-scatter.2.cloned.1.call-update) | async-done | bytes 262160 | tf_op jit(solution)/shard_map/reduce_scatter | solution.py:80
  156.2 1.7 %add_convert_fusion = bf16[64,2048]{1,0:T(8,128)(2,1)} fusion(f32[64,2048]{1,0:T(8,128)S(1)} %get-tuple-element.16, bf16[64,2048]{1,0:T(8,128)(2,1)} %reduce-scatter.2.cloned.1.call-done), kind=kLoop, calls=%fused_computation.38 | loop fusion | flops 393216 | bytes 1048576 | tf_op jit(solution)/shard_map/convert_element_type | solution.py:81
  157.9 0.0 copy-done.1
  (11 shorter events, 0.2 us)
Async XLA Ops:
  7.2 3.5 %copy-start = (bf16[2048,576]{0,1:T(8,128)(2,1)S(1)}, bf16[2048,576]{0,1:T(8,128)(2,1)}, u32[]{:S(2)}) copy-start(bf16[2048,576]{0,1:T(8,128)(2,1)} %param.21) | copy-start | bytes 7077892
  7.2 5.4 %copy-start.2 = (bf16[64,2048]{1,0:T(8,128)(2,1)S(1)}, bf16[64,2048]{1,0:T(8,128)(2,1)}, u32[]{:S(2)}) copy-start(bf16[64,2048]{1,0:T(8,128)(2,1)} %param.15) | copy-start | bytes 786436
  7.2 91.7 %all-gather.2.cloned.1.call-start = ((), (), s32[]{:S(2)}) async-start(), calls=%async_computation.1 | async-start | bytes 2359296 | tf_op jit(solution)/shard_map/all_gather | solution.py:75
  19.5 0.7 copy-start.5
  19.5 0.7 copy-start.4
  20.4 3.2 %copy-start.3 = (bf16[64,512]{1,0:T(8,128)(2,1)}, bf16[64,512]{1,0:T(8,128)(2,1)S(1)}, u32[]{:S(2)}) copy-start(bf16[64,512]{1,0:T(8,128)(2,1)S(1)} %get-tuple-element.4) | copy-start | bytes 196612
  66.9 89.3 %reduce-scatter.2.cloned.1.call-start = ((), (), s32[]{:S(2)}) async-start(), calls=%async_computation.2 | async-start | bytes 2359296 | tf_op jit(solution)/shard_map/reduce_scatter | solution.py:80
  106.8 51.0 %copy-start.1 = (bf16[2048,576]{0,1:T(8,128)(2,1)S(1)}, bf16[2048,576]{0,1:T(8,128)(2,1)}, u32[]{:S(2)}) copy-start(bf16[2048,576]{0,1:T(8,128)(2,1)} %param.21) | copy-start | bytes 7077892
Sparse Core Ops, SparseCore 0:
  67.0 31.8 all-gather.1
  120.9 35.2 reduce-scatter.1
where the time goes:
time: 165 us
  matrix products  74.9 us (45%)
  waiting for transfers between devices  66.5 us (40%)
  between operations  14.3 us (9%)
  other arithmetic  7.98 us (5%)
    reduce_scatter x1, waiting for transfers between devices, device_step(): lax.psum_scatter(partial_out, 'tp', scatter_dimension=0, tiled=True)  34.7 us
    all_gather x1, waiting for transfers between devices, device_step(): group_in = lax.all_gather(mlp_in, 'tp', axis=0, tiled=True)  31.7 us
    dot_general x1, matrix products, attention_block(): jnp.einsum('bhk,bsk->bhs', q_lat, cache_lat, preferred_element_type=jnp.f...  14.6 us
    dot_general x1, matrix products, attention_block(): jnp.einsum('bhs,bsk->bhk', probs, cache_lat, preferred_element_type=jnp.f...  14.3 us
    dot_general x1, matrix products, device_step(): jnp.dot(act, w_down, preferred_element_type=jnp.float32)  13.9 us
    dot_general x1, matrix products, device_step(): gate_proj = jnp.dot(group_in, w_gate, preferred_element_type=jnp.float32)  7.91 us
    dot_general x1, matrix products, attention_block(): jnp.dot(normed, w_query, preferred_element_type=jnp.float32)  6.95 us
    dot_general x1, matrix products, attention_block(): attn_out = jnp.dot(head_out, w_out, preferred_element_type=jnp.float32)  5.07 us
  transfers between devices with their start and end apart: 2, of which 2 were waited for; matrix products, arithmetic and copies ran while one was open for 0% of the time, Pallas kernels for 0%

commit v1 on v0

--- a/solution.py
+++ b/solution.py
@@ -1,6 +1,8 @@
 import jax
 import jax.numpy as jnp
 from jax import lax
+from jax.experimental import pallas as pl
+from jax.experimental.pallas import tpu as pltpu
 from jax.sharding import PartitionSpec as P
 
 EPS = 1e-6
@@ -62,6 +64,276 @@
     return resid, lat_new, rope_new
 
 
+MESH = pl.DeviceIdType.MESH
+NSUB = 2
+NRS = 4
+STRIP = 256
+
+
+def mlp_kernel(g_ref, resid_ref, wg_hbm, wu_hbm, wd_hbm, out_ref,
+               g_all, wg, wu, wd, act, pown, psend, precv, rsend, rrecv_e, rrecv_m,
+               w_sem, ag_recv, ag_recv_d, ag_send_e, ag_send_m, ag_send_d,
+               rd_recv, rd_send, rs_recv_e, rs_recv_m, rs_send):
+    ffn = wg.shape[0]
+    rows, width = g_ref.shape
+    sub = rows // NSUB
+    rsub = rows // NRS
+    me = lax.axis_index('tp')
+    z = lax.div(me, 2)
+    c = lax.rem(me, 2)
+    upper = z >= 2
+    is_end = jnp.logical_or(z == 0, z == 3)
+    is_int = jnp.logical_not(is_end)
+
+    def mir(k):
+        return jnp.where(upper, k, 3 - k)
+
+    partner = 2 * z + (1 - c)
+    dev_e = jnp.where(is_end, me, 2 * mir(3) + c)
+    dev_m = 2 * jnp.where(is_end, mir(2), mir(1)) + c
+
+    w_copies = []
+    for idx, (src, dst) in enumerate(((wg_hbm, wg), (wu_hbm, wu), (wd_hbm, wd))):
+        copy = pltpu.make_async_copy(src, dst, w_sem.at[idx])
+        copy.start()
+        w_copies.append(copy)
+
+    barrier = pltpu.get_barrier_semaphore()
+    pl.semaphore_signal(barrier, inc=1, device_id={'tp': partner}, device_id_type=MESH)
+    pl.semaphore_signal(barrier, inc=1, device_id={'tp': dev_m}, device_id_type=MESH)
+
+    @pl.when(is_int)
+    def _():
+        pl.semaphore_signal(barrier, inc=1, device_id={'tp': dev_e}, device_id_type=MESH)
+        pl.semaphore_wait(barrier, 3)
+
+    @pl.when(is_end)
+    def _():
+        pl.semaphore_wait(barrier, 2)
+
+    def remote(src, dst, send_sem, recv_sem, dev):
+        return pltpu.make_async_remote_copy(src_ref=src, dst_ref=dst, send_sem=send_sem, recv_sem=recv_sem, device_id={'tp': dev}, device_id_type=MESH)
+
+    def ag_copy(src, chip, k, send_sem, dev):
+        return remote(src, g_all.at[chip, 0, pl.ds(k * sub, sub)], send_sem.at[chip, k], ag_recv.at[chip, k], dev)
+
+    def ag_d2d(src, chip, k):
+        return remote(src, g_all.at[chip, 1, pl.ds(k * sub, sub)], ag_send_d.at[chip, k], ag_recv_d.at[chip, k], partner)
+
+    for k in range(NSUB):
+        piece = g_ref.at[pl.ds(k * sub, sub)]
+        ag_copy(piece, z, k, ag_send_m, dev_m).start()
+
+        @pl.when(is_int)
+        def _():
+            ag_copy(piece, z, k, ag_send_e, dev_e).start()
+
+        ag_d2d(piece, z, k).start()
+    g_all[z, 0] = g_ref[...]
+
+    def landed(chip, k):
+        return g_all.at[chip, 0, pl.ds(k * sub, sub)]
+
+    def arrive(chip, k, send_sem, dev):
+        src = landed(chip, k)
+        ag_copy(src, chip, k, ag_send_d, dev_m).wait_recv()
+        if dev is not None:
+            ag_copy(src, chip, k, send_sem, dev).start()
+        ag_d2d(src, chip, k).start()
+
+    def both(chip):
+        for k in range(NSUB):
+            ag_d2d(landed(chip, k), chip, k).wait_recv()
+
+    def rd_copy(chip):
+        return remote(psend.at[chip], precv.at[chip], rd_send.at[chip], rd_recv.at[chip], partner)
+
+    def rs_copy(chip, k, dst, recv_sem, dev):
+        span = pl.ds(k * rsub, rsub)
+        return remote(rsend.at[chip, span], dst.at[chip, span], rs_send.at[chip, k], recv_sem.at[chip, k], dev)
+
+    def rs_base(chip, k):
+        span = pl.ds(k * rsub, rsub)
+        return pown[chip, span] + precv[chip, span].astype(jnp.float32)
+
+    def end_send(chip):
+        rd_copy(chip).wait_recv()
+        for k in range(NRS):
+            rsend[chip, pl.ds(k * rsub, rsub)] = rs_base(chip, k).astype(jnp.bfloat16)
+            rs_copy(chip, k, rrecv_e, rs_recv_e, dev_m).start()
+
+    def hook(step, strip):
+        def at(role, want_step, want_strip, fn):
+            pl.when(jnp.logical_and(role, jnp.logical_and(step == want_step, strip == want_strip)))(fn)
+
+        def int_a():
+            arrive(mir(3), 1, ag_send_m, dev_m)
+            arrive(mir(1), 1, ag_send_e, dev_e)
+
+        at(is_int, 0, 2, int_a)
+        at(is_int, 1, 2, lambda: arrive(mir(0), 0, ag_send_e, dev_e))
+        at(is_int, 2, 1, lambda: arrive(mir(0), 1, ag_send_e, dev_e))
+        at(is_end, 0, 2, lambda: arrive(mir(2), 0, None, None))
+        at(is_end, 1, 2, lambda: arrive(mir(1), 0, None, None))
+        at(is_end, 2, 0, lambda: end_send(mir(2)))
+        at(is_end, 2, 2, lambda: arrive(mir(0), 0, None, None))
+        at(is_end, 3, 0, lambda: end_send(mir(1)))
+
+    def swiglu(lhs, at, count):
+        gate = lax.dot_general(lhs, wg[pl.ds(at, count)], (((1,), (1,)), ((), ())), preferred_element_type=jnp.float32)
+        up = lax.dot_general(lhs, wu[pl.ds(at, count)], (((1,), (1,)), ((), ())), preferred_element_type=jnp.float32)
+        return (gate / (1.0 + jnp.exp(-gate)) * up).astype(jnp.bfloat16)
+
+    whole = ffn // STRIP
+    rest = ffn - whole * STRIP
+
+    def one_step(step, carry):
+        third = jnp.where(is_end, mir(1), mir(1))
+        chip = jnp.where(step == 0, z, jnp.where(step == 1, jnp.where(is_end, mir(2), mir(3)), jnp.where(step == 2, third, mir(0))))
+
+        @pl.when(jnp.logical_and(step == 0, is_int))
+        def _():
+            arrive(mir(3), 0, ag_send_m, dev_m)
+            arrive(mir(1), 0, ag_send_e, dev_e)
+
+        @pl.when(jnp.logical_and(step == 2, is_end))
+        def _():
+            arrive(mir(1), 1, None, None)
+
+        @pl.when(jnp.logical_and(step == 3, is_end))
+        def _():
+            arrive(mir(0), 1, None, None)
+
+        both(chip)
+
+        @pl.when(step == 0)
+        def _():
+            w_copies[0].wait()
+            w_copies[1].wait()
+
+        def one_strip(strip, carry):
+            at = pl.multiple_of(strip * STRIP, STRIP)
+            act[:, pl.ds(at, STRIP)] = swiglu(g_all[chip].reshape(2 * rows, width), at, STRIP)
+            hook(step, strip)
+            return carry
+
+        lax.fori_loop(0, whole, one_strip, 0)
+        act[:, whole * STRIP:] = swiglu(g_all[chip].reshape(2 * rows, width), whole * STRIP, rest)
+
+        @pl.when(jnp.logical_and(step == 0, is_end))
+        def _():
+            arrive(mir(2), 1, None, None)
+
+        @pl.when(step == 0)
+        def _():
+            w_copies[2].wait()
+
+        def one_col(col, carry):
+            span = pl.ds(pl.multiple_of(col * STRIP, STRIP), STRIP)
+            part = jnp.dot(act[...], wd[:, span], preferred_element_type=jnp.float32)
+            pown[chip, :, span] = part[:rows]
+            psend[chip, :, span] = part[rows:].astype(jnp.bfloat16)
+            return carry
+
+        lax.fori_loop(0, width // STRIP, one_col, 0)
+        rd_copy(chip).start()
+        return carry
+
+    lax.fori_loop(0, 4, one_step, 0)
+
+    @pl.when(is_end)
+    def _():
+        end_send(mir(0))
+        rd_copy(z).wait_recv()
+        base = pown[z] + precv[z].astype(jnp.float32) + resid_ref[...].astype(jnp.float32)
+        pown[z] = base
+        for k in range(NRS):
+            span = pl.ds(k * rsub, rsub)
+            rs_copy(z, k, rrecv_m, rs_recv_m, dev_m).wait_recv()
+            out_ref[span] = (pown[z, span] + rrecv_m[z, span].astype(jnp.float32)).astype(jnp.bfloat16)
+
+    @pl.when(is_int)
+    def _():
+        def pass_on(chip, dst_in, sem_in, dst_out, sem_out, dev):
+            rd_copy(chip).wait_recv()
+            for k in range(NRS):
+                span = pl.ds(k * rsub, rsub)
+                rs_copy(chip, k, dst_in, sem_in, dev_m).wait_recv()
+                rsend[chip, span] = (rs_base(chip, k) + dst_in[chip, span].astype(jnp.float32)).astype(jnp.bfloat16)
+                rs_copy(chip, k, dst_out, sem_out, dev).start()
+
+        def own_send(chip):
+            pass_on(chip, rrecv_e, rs_recv_e, rrecv_m, rs_recv_m, dev_m)
+
+        own_send(mir(1))
+        rd_copy(z).wait_recv()
+        for k in range(NRS):
+            rs_copy(z, k, rrecv_e, rs_recv_e, dev_m).wait_recv()
+        pown[z] = pown[z] + precv[z].astype(jnp.float32) + resid_ref[...].astype(jnp.float32) + rrecv_e[z].astype(jnp.float32)
+        own_send(mir(0))
+        for k in range(NRS):
+            span = pl.ds(k * rsub, rsub)
+            rs_copy(z, k, rrecv_m, rs_recv_m, dev_m).wait_recv()
+            out_ref[span] = (pown[z, span] + rrecv_m[z, span].astype(jnp.float32)).astype(jnp.bfloat16)
+        pass_on(mir(3), rrecv_m, rs_recv_m, rrecv_m, rs_recv_m, dev_e)
+
+    for k in range(NSUB):
+        for chip in range(4):
+            ag_d2d(landed(chip, k), chip, k).wait_send()
+        ag_copy(landed(z, k), z, k, ag_send_m, dev_m).wait_send()
+
+        @pl.when(is_int)
+        def _():
+            ag_copy(landed(z, k), z, k, ag_send_e, dev_e).wait_send()
+            ag_copy(landed(mir(3), k), mir(3), k, ag_send_m, dev_m).wait_send()
+            ag_copy(landed(mir(1), k), mir(1), k, ag_send_e, dev_e).wait_send()
+            ag_copy(landed(mir(0), k), mir(0), k, ag_send_e, dev_e).wait_send()
+
+    for chip in range(4):
+        rd_copy(chip).wait_send()
+
+        @pl.when(chip != z)
+        def _():
+            for k in range(NRS):
+                rs_copy(chip, k, rrecv_m, rs_recv_m, dev_m).wait_send()
+
+
+def mlp_block(mlp_in, resid, w_gate_t, w_up_t, w_down):
+    rows, width = mlp_in.shape
+    ffn = w_gate_t.shape[0]
+    bf16, f32 = jnp.bfloat16, jnp.float32
+    vmem = pl.BlockSpec(memory_space=pltpu.VMEM)
+    hbm = pl.BlockSpec(memory_space=pl.ANY)
+    dma = pltpu.SemaphoreType.DMA
+    flops = 3 * 2 * 8 * rows * width * ffn
+    return pl.pallas_call(
+        mlp_kernel,
+        out_shape=jax.ShapeDtypeStruct((rows, width), bf16),
+        in_specs=[vmem, vmem, hbm, hbm, hbm],
+        out_specs=vmem,
+        scratch_shapes=[
+            pltpu.VMEM((4, 2, rows, width), bf16),
+            pltpu.VMEM((ffn, width), bf16),
+            pltpu.VMEM((ffn, width), bf16),
+            pltpu.VMEM((ffn, width), bf16),
+            pltpu.VMEM((2 * rows, ffn), bf16),
+            pltpu.VMEM((4, rows, width), f32),
+            pltpu.VMEM((4, rows, width), bf16),
+            pltpu.VMEM((4, rows, width), bf16),
+            pltpu.VMEM((4, rows, width), bf16),
+            pltpu.VMEM((4, rows, width), bf16),
+            pltpu.VMEM((4, rows, width), bf16),
+            dma((3,)),
+            dma((4, NSUB)), dma((4, NSUB)), dma((4, NSUB)), dma((4, NSUB)), dma((4, NSUB)),
+            dma((4,)), dma((4,)),
+            dma((4, NRS)), dma((4, NRS)), dma((4, NRS)),
+        ],
+        compiler_params=pltpu.CompilerParams(collective_id=0, has_side_effects=True, vmem_limit_bytes=60 * 1024 * 1024),
+        cost_estimate=pl.CostEstimate(flops=flops, bytes_accessed=3 * 2 * ffn * width, transcendentals=8 * rows * ffn),
+        name='mlp_exchange',
+    )(mlp_in, resid, w_gate_t, w_up_t, w_down)
+
+
 def solution(mesh):
     rows_spec = P(('dp', 'tp'), None)
     cache_spec = P(('dp', 'tp'), None, None)
@@ -72,13 +344,7 @@
     def device_step(hidden, cache_lat, cache_rope, seq_lens, attn_norm, w_query, w_kv_down, kv_norm, w_key_up, w_val_up, w_out, mlp_norm, w_gate, w_up, w_down):
         resid, lat_new, rope_new = attention_block(hidden, cache_lat, cache_rope, seq_lens, attn_norm, w_query, w_kv_down, kv_norm, w_key_up, w_val_up, w_out)
         mlp_in = rms_norm(resid, mlp_norm)
-        group_in = lax.all_gather(mlp_in, 'tp', axis=0, tiled=True)
-        gate_proj = jnp.dot(group_in, w_gate, preferred_element_type=jnp.float32)
-        up_proj = jnp.dot(group_in, w_up, preferred_element_type=jnp.float32)
-        act = (jax.nn.silu(gate_proj) * up_proj).astype(jnp.bfloat16)
-        partial_out = jnp.dot(act, w_down, preferred_element_type=jnp.float32).astype(jnp.bfloat16)
-        mlp_out = lax.psum_scatter(partial_out, 'tp', scatter_dimension=0, tiled=True)
-        out_hidden = (resid.astype(jnp.float32) + mlp_out.astype(jnp.float32)).astype(jnp.bfloat16)
+        out_hidden = mlp_block(mlp_in, resid, w_gate.T, w_up.T, w_down)
         return out_hidden, lat_new, rope_new
 
     return jax.shard_map(device_step, mesh=mesh, in_specs=in_specs, out_specs=out_specs, check_vma=False)

time: 165 us -> 123 us (0.75)
  waiting for transfers between devices: 66.5 us -> 0 us
  Pallas kernels: 0 us -> 59.5 us
  matrix products: 74.9 us -> 51.5 us
  between operations: 14.3 us -> 0.85 us
  local copies, waits for them, and re-layouts: 0.75 us -> 3.35 us
    pallas_call x0 -> x1, Pallas kernels: none -> 59.5 us  [mlp_block(): pl.pallas_call(mlp_kernel, out_shape=jax.ShapeDtypeStruct((rows, width),...]
    reduce_scatter x1 -> x0, waiting for transfers between devices: 34.7 us -> none  [device_step(): lax.psum_scatter(partial_out, 'tp', scatter_dimension=0, tiled=True)]
    all_gather x1 -> x0, waiting for transfers between devices: 31.7 us -> none  [device_step(): group_in = lax.all_gather(mlp_in, 'tp', axis=0, tiled=True)]
    dot_general x2 -> x0, matrix products: 21.8 us -> none  [the longest x1 13.9 us: device_step(): jnp.dot(act, w_down, preferred_element_type=jnp.float32)]
    unnamed x12 -> x13, local copies, waits for them, and re-layouts: 0.04 us -> 2.63 us
    convert_element_type x1 -> x0, other arithmetic: 1.7 us -> none  [device_step(): (resid.astype(jnp.float32) + mlp_out.astype(jnp.float32)).astype(jnp.bflo...]
  transfers between devices with their start and end apart: 2 -> 0, of which waited for: 2 -> 0; matrix products, arithmetic and copies ran while one was open for 0% -> 0% of each run, Pallas kernels for 0% -> 0%
where the time goes in v1:
time: 123 us
  Pallas kernels  59.5 us (48%)
  matrix products  51.5 us (42%)
  other arithmetic  7.64 us (6%)
  local copies, waits for them, and re-layouts  3.35 us (3%)
    pallas_call x1, Pallas kernels, mlp_block(): pl.pallas_call(mlp_kernel, out_shape=jax.ShapeDtypeStruct((rows, width),...  59.5 us
    dot_general x1, matrix products, attention_block(): jnp.einsum('bhk,bsk->bhs', q_lat, cache_lat, preferred_element_type=jnp.f...  14.6 us
    dot_general x1, matrix products, attention_block(): jnp.einsum('bhs,bsk->bhk', probs, cache_lat, preferred_element_type=jnp.f...  14.3 us
    dot_general x1, matrix products, attention_block(): jnp.dot(normed, w_query, preferred_element_type=jnp.float32)  6.97 us
    dot_general x1, matrix products, attention_block(): attn_out = jnp.dot(head_out, w_out, preferred_element_type=jnp.float32)  5.08 us
    dot_general x1, matrix products, attention_block(): jnp.einsum('bhk,khv->bhv', lat_out, val_up, preferred_element_type=jnp.fl...  3.8 us
    dot_general x1, matrix products, attention_block(): jnp.einsum('bhr,bsr->bhs', q_rot, cache_rope, preferred_element_type=jnp....  3.16 us
    convert_element_type x4, other arithmetic, rms_norm(): return (vals32 * inv_rms * gain.astype(jnp.float32)).astype(jnp.bfloat16)  2.9 us

profile of v1, /device:TPU:0, one launch (start us, length us, event | category | flops | bytes accessed | tf_op | source)
XLA Modules:
  0.0 122.8 jit_solution(12658052537454254051)
XLA Ops:
  0.6 0.0 copy-start
  0.6 0.0 copy-start.2
  0.7 0.8 convert_element_type.82
  1.5 1.1 fusion.34
  2.6 0.7 convert_element_type.85
  3.3 0.7 convert_element_type.76
  4.0 0.7 convert_element_type.97
  4.7 0.7 iota_compare_fusion
  5.4 0.0 copy-done
  5.4 1.8 %convolution_convert_fusion.1 = bf16[64,576]{1,0:T(8,128)(2,1)S(1)} fusion(bf16[2048,576]{0,1:T(8,128)(2,1)S(1)} %copy-done, bf16[64,2048]{1,0:T(8,128)(2,1)} %param.15, f32[2048]{0:T(1024)S(1)} %convert_element_type.76, f32[64]{0:T(128)S(1)} %add_rsqrt_fusion.2), kind=kOutput, calls=%fused_computation.19 | convolution fusion | flops 151556096 | bytes 2703616 | tf_op jit(solution)/shard_map/dot_general | solution.py:40
  7.2 0.1 fusion.40
  7.3 0.2 subtract_convert_fusion.1
  7.5 0.1 fusion.62
  7.6 0.7 pad_maximum_fusion.3
  8.3 0.1 fusion.53
  8.4 0.0 copy-start.5
  8.4 0.0 copy-done.2
  8.4 7.0 %convolution_convert_fusion = bf16[64,3072]{1,0:T(8,128)(2,1)S(1)} fusion(bf16[2048,3072]{1,0:T(8,128)(2,1)} %param.20, bf16[64,2048]{1,0:T(8,128)(2,1)S(1)} %copy-done.2, f32[2048]{0:T(1024)S(1)} %convert_element_type.76, f32[64]{0:T(128)S(1)} %add_rsqrt_fusion.2), kind=kOutput, calls=%fused_computation | convolution fusion | flops 806027264 | bytes 13246720 | tf_op jit(solution)/shard_map/dot_general | solution.py:39
  15.4 0.6 reshape.122
  16.0 0.0 copy-start.3
  16.1 0.2 subtract_convert_fusion
  16.4 0.3 fusion.46
  16.7 0.9 copy-done.3
  17.6 0.8 fusion.12
  18.5 0.0 copy-done.5
  18.5 0.7 fusion.27
  19.2 14.6 %fusion.29 = f32[64,16,512]{2,1,0:T(8,128)S(1)} fusion(bf16[64,512,512]{2,1,0:T(8,128)(2,1)} %param.16, bf16[64,16,512]{2,0,1:T(8,128)(2,1)S(1)} %fusion.12), kind=kOutput, calls=%fused_computation.27 | convolution fusion | flops 536870912 | bytes 36700160 | tf_op jit(solution)/shard_map/bhk,bsk->bhs/dot_general | solution.py:47
  33.8 3.2 %fusion.55 = (f32[64,16]{1,0:T(8,128)S(1)}, f32[64,16,512]{2,1,0:T(8,128)S(1)}) fusion(f32[64,16,512]{2,1,0:T(8,128)S(1)} %fusion.29, bf16[64,512,64]{1,2,0:T(8,128)(2,1)} %param.17, bf16[64,16,32]{2,1,0:T(8,128)(2,1)S(1)} %get-tuple-element.6, bf16[64,16,32]{2,1,0:T(8,128)(2,1)S(1)} %get-tuple-element.5, pred[64,512]{1,0:T(8,128)(4,1)S(1)} %iota_compare_fusion), kind=kOutput, calls=%fused_computation.74 | convolution fusion | flops 69467136 | bytes 8556544 | tf_op jit(solution)/shard_map/bhr,bsr->bhs/dot_general | solution.py:47
  37.0 0.6 fusion.8
  37.6 14.3 %fusion.21 = f32[64,16,512]{2,1,0:T(8,128)} fusion(bf16[64,512,512]{2,1,0:T(8,128)(2,1)} %param.16, f32[64,16,512]{2,1,0:T(8,128)S(1)} %get-tuple-element.14, f32[64,16]{1,0:T(8,128)S(1)} %get-tuple-element.8, f32[64,16]{1,0:T(8,128)S(1)} %fusion.49), kind=kOutput, calls=%fused_computation.20 | convolution fusion | flops 538443776 | bytes 37756928 | tf_op jit(solution)/shard_map/bhs,bsk->bhk/dot_general | solution.py:58
  51.9 0.1 copy.26
  51.9 3.8 %fusion.18 = bf16[16,8,8,128]{3,2,1,0:T(8,128)(2,1)S(1)} fusion(f32[64,16,512]{2,1,0:T(8,128)} %fusion.21, f32[64,512]{1,0:T(8,128)S(1)} %get-tuple-element.3, f32[64,16]{0,1:T(8,128)S(1)} %copy.26, bf16[512,2048]{1,0:T(8,128)(2,1)} %param.24), kind=kOutput, calls=%fused_computation.18 | convolution fusion | flops 135921664 | bytes 4591616 | tf_op jit(solution)/shard_map/bhk,khv->bhv/dot_general | solution.py:61
  55.7 5.1 %fusion.31 = (f32[64]{0:T(128)S(1)}, bf16[64,2048]{1,0:T(8,128)(2,1)S(1)}) fusion(bf16[2048,2048]{1,0:T(8,128)(2,1)} %param.25, bf16[16,8,8,128]{3,2,1,0:T(8,128)(2,1)S(1)} %fusion.18, bf16[64,2048]{1,0:T(8,128)(2,1)S(1)} %copy-done.2), kind=kOutput, calls=%fused_computation.33 | convolution fusion | flops 537657280 | bytes 9175296 | tf_op jit(solution)/shard_map/dot_general | solution.py:62
  60.8 0.0 copy-start.4
  60.8 0.8 fusion.33.g_ref
  61.7 0.0 copy-done.4
  61.7 0.0 copy-start.1
  61.7 59.5 %mlp_exchange.1 = bf16[64,2048]{1,0:T(8,128)(2,1)} custom-call(bf16[64,2048]{1,0:T(8,128)(2,1)} %fusion.33.g_ref, bf16[64,2048]{1,0:T(8,128)(2,1)} %copy-done.4, bf16[1368,2048]{1,0:T(8,128)(2,1)} %bitcast.52, bf16[1368,2048]{1,0:T(8,128)(2,1)} %bitcast.53, bf16[1368,2048]{1,0:T(8,128)(2,1)} %wd_hbm.1), custom_call_target="tpu_custom_call" | custom-call | flops 8606711808 | bytes 16809984 | tf_op jit(solution)/shard_map/mlp_exchange/pallas_call | solution.py:309
  121.2 1.7 %copy.75 = bf16[64,2048]{1,0:T(8,128)(2,1)} copy(bf16[64,2048]{1,0:T(8,128)(2,1)} %mlp_exchange.1) | data formatting | bytes 524288
  122.8 0.0 copy-done.1
  (9 shorter events, 0.2 us)
Async XLA Ops:
  0.6 4.8 %copy-start = (bf16[2048,576]{0,1:T(8,128)(2,1)S(1)}, bf16[2048,576]{0,1:T(8,128)(2,1)}, u32[]{:S(2)}) copy-start(bf16[2048,576]{0,1:T(8,128)(2,1)} %param.21) | copy-start | bytes 7077892
  0.6 7.8 %copy-start.2 = (bf16[64,2048]{1,0:T(8,128)(2,1)S(1)}, bf16[64,2048]{1,0:T(8,128)(2,1)}, u32[]{:S(2)}) copy-start(bf16[64,2048]{1,0:T(8,128)(2,1)} %param.15) | copy-start | bytes 786436
  8.4 10.1 %copy-start.5 = (bf16[64,512]{1,0:T(8,128)(2,1)}, bf16[64,512]{1,0:T(8,128)(2,1)S(1)}, u32[]{:S(2)}) copy-start(bf16[64,512]{1,0:T(8,128)(2,1)S(1)} %get-tuple-element.21) | copy-start | bytes 196612
  16.0 1.6 %copy-start.3 = (bf16[512,2048]{1,0:T(8,128)(2,1)S(1)}, bf16[512,2048]{1,0:T(8,128)(2,1)}, u32[]{:S(2)}) copy-start(bf16[512,2048]{1,0:T(8,128)(2,1)} %param.23) | copy-start | bytes 6291460
  60.8 0.9 copy-start.4
  61.7 61.2 %copy-start.1 = (bf16[2048,576]{0,1:T(8,128)(2,1)S(1)}, bf16[2048,576]{0,1:T(8,128)(2,1)}, u32[]{:S(2)}) copy-start(bf16[2048,576]{0,1:T(8,128)(2,1)} %param.21) | copy-start | bytes 7077892

commit v2 on v1

--- a/solution.py
+++ b/solution.py
@@ -1,3 +1,5 @@
+import math
+
 import jax
 import jax.numpy as jnp
 from jax import lax
@@ -7,61 +9,251 @@
 
 EPS = 1e-6
 ROPE_BASE = 10000.0
-value_a7 = 512
 ROPE_DIM = 64
 NOPE_DIM = 128
+VAL_DIM = 128
 SCALE = (NOPE_DIM + ROPE_DIM) ** -0.5
 
 
-def rms_norm(vals, gain):
-    vals32 = vals.astype(jnp.float32)
-    inv_rms = lax.rsqrt(jnp.mean(vals32 * vals32, axis=-1, keepdims=True) + EPS)
-    return (vals32 * inv_rms * gain.astype(jnp.float32)).astype(jnp.bfloat16)
-
-
-def rotate(vals, cos_tab, sin_tab):
-    half = vals.shape[-1] // 2
-    first = vals[..., :half]
-    second = vals[..., half:]
-    return jnp.concatenate([first * cos_tab - second * sin_tab, second * cos_tab + first * sin_tab], axis=-1)
-
-
-def rope_tables(seq_lens):
-    inv_freq = ROPE_BASE ** (-jnp.arange(0, ROPE_DIM, 2, dtype=jnp.float32) / ROPE_DIM)
-    angles = seq_lens.astype(jnp.float32)[:, None] * inv_freq[None, :]
-    return jnp.cos(angles), jnp.sin(angles)
-
-
-def attention_block(hidden, cache_lat, cache_rope, seq_lens, attn_norm, w_query, w_kv_down, kv_norm, w_key_up, w_val_up, w_out):
-    rows = hidden.shape[0]
+GROUP = 4
+SLOTS = 7
+BLOCK = 128
+Q_CHUNKS = 4
+VMEM_LIMIT = 63 * 1024 * 1024
+
+
+def attn_kernel(lens_ref, hidden_ref, lens_col, attn_gain, kv_gain, mlp_gain, lat_hbm, rope_hbm, wq_hbm, wkv_hbm, wk_hbm, wv_hbm, wo_hbm,
+                resid_ref, mlp_in_ref, lat_new_ref, rope_new_ref,
+                keys, rope, wq, wkv, wk, wv, wo, normed, qs, qr, lat_row, rope_row, heads_out, order, key_sem, w_sem):
+    f32, bf16 = jnp.float32, jnp.bfloat16
+    rows, width = hidden_ref.shape
+    rank = wk.shape[0]
+    heads = wk.shape[1] // NOPE_DIM
+    groups = rows // GROUP
+    classes = keys.shape[2] // BLOCK
+
+    chunk = wq.shape[2]
+    w_copies = [pltpu.make_async_copy(wkv_hbm, wkv, w_sem.at[0]), pltpu.make_async_copy(wk_hbm, wk, w_sem.at[1])]
+    w_copies += [pltpu.make_async_copy(wq_hbm.at[:, pl.ds(j * chunk, chunk)], wq.at[j], w_sem.at[2 + j]) for j in range(Q_CHUNKS)]
+    rope_copy = pltpu.make_async_copy(rope_hbm, rope, w_sem.at[2 + Q_CHUNKS])
+    late_copies = [pltpu.make_async_copy(wv_hbm, wv, w_sem.at[3 + Q_CHUNKS]), pltpu.make_async_copy(wo_hbm, wo, w_sem.at[4 + Q_CHUNKS])]
+    for copy in w_copies:
+        copy.start()
+    rope_copy.start()
+
+    def kind(b):
+        return lax.div(lens_ref[b], BLOCK)
+
+    def count(b, counts):
+        k = kind(b)
+        return tuple(n + jnp.where(k == i, 1, 0) for i, n in enumerate(counts))
+
+    zero = jnp.int32(0)
+    counts = lax.fori_loop(0, rows, count, (zero,) * classes)
+    firsts = []
+    total = zero
+    for i in reversed(range(classes)):
+        firsts.append(total)
+        total = total + counts[i]
+    firsts = tuple(reversed(firsts))
+
+    def place(b, firsts):
+        k = kind(b)
+        at = firsts[0]
+        for i in range(1, classes):
+            at = jnp.where(k == i, firsts[i], at)
+        order[at] = b
+        return tuple(n + jnp.where(k == i, 1, 0) for i, n in enumerate(firsts))
+
+    lax.fori_loop(0, rows, place, firsts)
+
+    def group_copies(g, blocks):
+        slot = lax.rem(g, SLOTS)
+        return [pltpu.make_async_copy(lat_hbm.at[order[g * GROUP + i], pl.ds(0, blocks * BLOCK)], keys.at[slot, i, pl.ds(0, blocks * BLOCK)], key_sem.at[slot, i]) for i in range(GROUP)]
+
+    def per_class(g, fn):
+        k = kind(order[g * GROUP])
+        for i in range(classes):
+            @pl.when(k == i)
+            def _():
+                fn(i + 1)
+
+    def start_group(g):
+        def start(blocks):
+            for copy in group_copies(g, blocks):
+                copy.start()
+
+        per_class(g, start)
+
+    def start_first(g, carry):
+        start_group(g)
+        return carry
+
+    lax.fori_loop(0, SLOTS, start_first, 0)
+
+    vals = hidden_ref[...].astype(f32)
+    inv_rms = lax.rsqrt(jnp.mean(vals * vals, axis=-1, keepdims=True) + EPS)
+    normed[...] = (vals * inv_rms * attn_gain[...].astype(f32)).astype(bf16)
+
+    lane = lax.broadcasted_iota(jnp.int32, (rows, 2 * ROPE_DIM), 1)
+    half = ROPE_DIM // 2
+    freq = jnp.exp(lax.rem(lane, half).astype(f32) * (-math.log(ROPE_BASE) / half))
+    angles = lens_col[...].astype(f32) * freq
+    cos_tab = jnp.cos(angles)
+    is_first = lax.rem(lane, ROPE_DIM) < half
+    sin_tab = jnp.where(is_first, -jnp.sin(angles), jnp.sin(angles))
+
+    def rotate_pair(pair):
+        swapped = jnp.where(is_first, pltpu.roll(pair, 2 * ROPE_DIM - half, 1), pltpu.roll(pair, half, 1))
+        return (pair * cos_tab + swapped * sin_tab).astype(bf16).astype(f32)
+
+    w_copies[0].wait()
+    kv = lax.dot_general(normed[...], wkv[...], (((1,), (1,)), ((), ())), preferred_element_type=f32).astype(bf16).astype(f32)
+    lat = kv[:, :rank]
+    inv_lat = lax.rsqrt(jnp.mean(lat * lat, axis=-1, keepdims=True) + EPS)
+    lat_new = (lat * inv_lat * kv_gain[...].astype(f32)).astype(bf16)
+    lat_new_ref[...] = lat_new
+    lat_row[...] = lat_new.astype(f32)
+    pe = kv[:, rank:]
+    rope_new = rotate_pair(jnp.concatenate([pe, pe], axis=1))
+    rope_new_ref[...] = rope_new[:, :ROPE_DIM].astype(bf16)
+    rope_row[...] = rope_new
+
+    w_copies[1].wait()
+    low = lane < ROPE_DIM
+
+    def put_head(head, nope, pe_rot):
+        key_up = wk[:, head * NOPE_DIM:(head + 1) * NOPE_DIM]
+        q_lat = lax.dot_general(nope.astype(bf16), key_up, (((1,), (1,)), ((), ())), preferred_element_type=f32).astype(bf16).astype(f32)
+        for part in range(rank // 128):
+            qs[part, pl.ds(head, rows, stride=heads), :] = q_lat[:, part * 128:(part + 1) * 128]
+        qr[pl.ds(head, rows, stride=heads), :] = pe_rot
+
+    for j in range(Q_CHUNKS):
+        w_copies[2 + j].wait()
+        query = jnp.dot(normed[...], wq[j], preferred_element_type=f32).astype(bf16).astype(f32)
+        for pair in range(chunk // 384):
+            base = pair * 384
+            part_a, part_b, part_c = (query[:, base + 128 * i:base + 128 * (i + 1)] for i in range(3))
+            pe_rot = rotate_pair(jnp.where(low, part_b, part_c))
+            head = (j * chunk + base) // 192
+            put_head(head, part_a, pe_rot)
+            put_head(head + 1, jnp.where(low, pltpu.roll(part_b, ROPE_DIM, 1), pltpu.roll(part_c, ROPE_DIM, 1)), pltpu.roll(pe_rot, ROPE_DIM, 1))
+
+    rope_copy.wait()
+
+    def attend(g, blocks):
+        slot = lax.rem(g, SLOTS)
+        span = blocks * BLOCK
+        for copy in group_copies(g, blocks):
+            copy.wait()
+        scores = []
+        picks = [order[g * GROUP + i] for i in range(GROUP)]
+        for i, b in enumerate(picks):
+            length = lens_ref[b]
+            base = pl.multiple_of(lax.div(length, 16) * 16, 16)
+            tile = keys[slot, i, pl.ds(base, 16), :].astype(f32)
+            sub = lax.broadcasted_iota(jnp.int32, (16, rank), 0)
+            keys[slot, i, pl.ds(base, 16), :] = jnp.where(sub == length - base, lat_row[pl.ds(b, 1), :], tile).astype(bf16)
+        for i, b in enumerate(picks):
+            length = lens_ref[b]
+            mine = pl.ds(pl.multiple_of(b * heads, heads), heads)
+            q_lat = jnp.concatenate([qs[part, mine, :] for part in range(rank // 128)], axis=1).astype(bf16)
+            q_rot = qr[mine, :]
+            score = lax.dot_general(q_lat, keys[slot, i, :span], (((1,), (1,)), ((), ())), preferred_element_type=f32)
+            near = jnp.dot(q_rot[:, :ROPE_DIM].astype(bf16), rope[b, :, :span], preferred_element_type=f32)
+            first = lax.broadcasted_iota(jnp.int32, (heads, 2 * ROPE_DIM), 1) < ROPE_DIM
+            new = jnp.sum(jnp.where(first, q_rot * rope_row[pl.ds(b, 1), :], 0.0), axis=1, keepdims=True)
+            at = lax.broadcasted_iota(jnp.int32, (heads, span), 1)
+            score = (score + jnp.where(at == length, new, near)) * SCALE
+            scores.append(jnp.where(at <= length, score, -jnp.inf))
+        probs = []
+        for score in scores:
+            expo = jnp.exp(score - jnp.max(score, axis=1, keepdims=True))
+            probs.append((expo / jnp.sum(expo, axis=1, keepdims=True)).astype(bf16))
+        for i, b in enumerate(picks):
+            mine = pl.ds(pl.multiple_of(b * heads, heads), heads)
+            out = jnp.dot(probs[i], keys[slot, i, :span], preferred_element_type=f32)
+            for part in range(rank // 128):
+                qs[part, mine, :] = out[:, part * 128:(part + 1) * 128]
+
+    def one_group(g, carry):
+        per_class(g, lambda blocks: attend(g, blocks))
+
+        @pl.when(g + SLOTS < groups)
+        def _():
+            start_group(g + SLOTS)
+
+        @pl.when(g == groups - SLOTS - 1)
+        def _():
+            for copy in late_copies:
+                copy.start()
+
+        return carry
+
+    lax.fori_loop(0, groups, one_group, 0)
+
+    late_copies[0].wait()
+    for head in range(heads):
+        cols = slice(head * VAL_DIM, (head + 1) * VAL_DIM)
+        lat_out = jnp.concatenate([qs[part, pl.ds(head, rows, stride=heads), :] for part in range(rank // 128)], axis=1).astype(bf16)
+        heads_out[:, cols] = jnp.dot(lat_out, wv[:, cols], preferred_element_type=f32).astype(bf16)
+    late_copies[1].wait()
+    square = jnp.zeros((rows, 1), f32)
+    for n in range(width // 512):
+        cols = slice(n * 512, (n + 1) * 512)
+        attn_out = jnp.dot(heads_out[...], wo[:, cols], preferred_element_type=f32)
+        resid = (hidden_ref[:, cols].astype(f32) + attn_out).astype(bf16)
+        resid_ref[:, cols] = resid
+        square = square + jnp.sum(resid.astype(f32) * resid.astype(f32), axis=-1, keepdims=True)
+    inv_rms = lax.rsqrt(square * (1.0 / width) + EPS)
+    mlp_in_ref[...] = (resid_ref[...].astype(f32) * inv_rms * mlp_gain[...].astype(f32)).astype(bf16)
+
+
+def attention_block(hidden, cache_lat, cache_rope, seq_lens, attn_norm, w_query, w_kv_down, kv_norm, w_key_up, w_val_up, w_out, mlp_norm):
+    rows, width = hidden.shape
+    slots, rank = cache_lat.shape[1:]
+    bf16, f32 = jnp.bfloat16, jnp.float32
     heads = w_key_up.shape[1] // NOPE_DIM
-    normed = rms_norm(hidden, attn_norm)
-    query = jnp.dot(normed, w_query, preferred_element_type=jnp.float32).astype(jnp.bfloat16).reshape(rows, heads, NOPE_DIM + ROPE_DIM)
-    kv_proj = jnp.dot(normed, w_kv_down, preferred_element_type=jnp.float32).astype(jnp.bfloat16)
-    lat_new = rms_norm(kv_proj[:, :value_a7], kv_norm)
-    cos_tab, sin_tab = rope_tables(seq_lens)
-    rope_new = rotate(kv_proj[:, value_a7:].astype(jnp.float32), cos_tab, sin_tab).astype(jnp.bfloat16)
-    q_rot = rotate(query[:, :, NOPE_DIM:].astype(jnp.float32), cos_tab[:, None, :], sin_tab[:, None, :]).astype(jnp.bfloat16)
-    key_up = w_key_up.reshape(value_a7, heads, NOPE_DIM)
-    q_lat = jnp.einsum('bhn,khn->bhk', query[:, :, :NOPE_DIM], key_up, preferred_element_type=jnp.float32).astype(jnp.bfloat16)
-    scores = (jnp.einsum('bhk,bsk->bhs', q_lat, cache_lat, preferred_element_type=jnp.float32) + jnp.einsum('bhr,bsr->bhs', q_rot, cache_rope, preferred_element_type=jnp.float32)) * SCALE
-    score_new = (jnp.einsum('bhk,bk->bh', q_lat, lat_new, preferred_element_type=jnp.float32) + jnp.einsum('bhr,br->bh', q_rot, rope_new, preferred_element_type=jnp.float32)) * SCALE
-    slots = cache_lat.shape[1]
-    valid = jnp.arange(slots)[None, None, :] < seq_lens[:, None, None]
-    scores = jnp.where(valid, scores, -jnp.inf)
-    top = jnp.maximum(jnp.max(scores, axis=-1), score_new)
-    expo = jnp.exp(scores - top[..., None])
-    expo_new = jnp.exp(score_new - top)
-    denom = jnp.sum(expo, axis=-1) + expo_new
-    probs = (expo / denom[..., None]).astype(jnp.bfloat16)
-    prob_new = (expo_new / denom).astype(jnp.bfloat16)
-    lat_sum = jnp.einsum('bhs,bsk->bhk', probs, cache_lat, preferred_element_type=jnp.float32) + prob_new.astype(jnp.float32)[..., None] * lat_new.astype(jnp.float32)[:, None, :]
-    lat_out = lat_sum.astype(jnp.bfloat16)
-    val_up = w_val_up.reshape(value_a7, heads, -1)
-    head_out = jnp.einsum('bhk,khv->bhv', lat_out, val_up, preferred_element_type=jnp.float32).astype(jnp.bfloat16).reshape(rows, -1)
-    attn_out = jnp.dot(head_out, w_out, preferred_element_type=jnp.float32)
-    resid = (hidden.astype(jnp.float32) + attn_out).astype(jnp.bfloat16)
-    return resid, lat_new, rope_new
+    q_width = w_query.shape[1]
+    vmem = pl.BlockSpec(memory_space=pltpu.VMEM)
+    hbm = pl.BlockSpec(memory_space=pl.ANY)
+    smem = pl.BlockSpec(memory_space=pltpu.SMEM)
+    dma = pltpu.SemaphoreType.DMA
+    flops = 2 * rows * (width * (q_width + rank + ROPE_DIM + width) + heads * rank * (NOPE_DIM + VAL_DIM) + heads * slots * (2 * rank + ROPE_DIM))
+    moved = 2 * (width * (q_width + rank + ROPE_DIM + width) + heads * rank * (NOPE_DIM + VAL_DIM) + rows * slots * (rank + ROPE_DIM))
+    return pl.pallas_call(
+        attn_kernel,
+        out_shape=(
+            jax.ShapeDtypeStruct((rows, width), bf16),
+            jax.ShapeDtypeStruct((rows, width), bf16),
+            jax.ShapeDtypeStruct((rows, rank), bf16),
+            jax.ShapeDtypeStruct((rows, ROPE_DIM), bf16),
+        ),
+        in_specs=[smem] + [vmem] * 5 + [hbm] * 7,
+        out_specs=(vmem,) * 4,
+        scratch_shapes=[
+            pltpu.VMEM((SLOTS, GROUP, slots, rank), bf16),
+            pltpu.VMEM((rows, ROPE_DIM, slots), bf16),
+            pltpu.VMEM((Q_CHUNKS, width, q_width // Q_CHUNKS), bf16),
+            pltpu.VMEM((rank + ROPE_DIM, width), bf16),
+            pltpu.VMEM((rank, heads * NOPE_DIM), bf16),
+            pltpu.VMEM((rank, heads * VAL_DIM), bf16),
+            pltpu.VMEM((heads * VAL_DIM, width), bf16),
+            pltpu.VMEM((rows, width), bf16),
+            pltpu.VMEM((rank // 128, rows * heads, 128), f32),
+            pltpu.VMEM((rows * heads, 2 * ROPE_DIM), f32),
+            pltpu.VMEM((rows, rank), f32),
+            pltpu.VMEM((rows, 2 * ROPE_DIM), f32),
+            pltpu.VMEM((rows, heads * VAL_DIM), bf16),
+            pltpu.SMEM((rows,), jnp.int32),
+            dma((SLOTS, GROUP)),
+            dma((5 + Q_CHUNKS,)),
+        ],
+        compiler_params=pltpu.CompilerParams(vmem_limit_bytes=VMEM_LIMIT),
+        cost_estimate=pl.CostEstimate(flops=flops, bytes_accessed=moved, transcendentals=rows * heads * slots),
+        name='latent_attention',
+    )(seq_lens, hidden, seq_lens[:, None], attn_norm[None], kv_norm[None], mlp_norm[None], cache_lat, jnp.swapaxes(cache_rope, 1, 2), w_query, w_kv_down.T, w_key_up, w_val_up, w_out)
 
 
 MESH = pl.DeviceIdType.MESH
@@ -342,8 +534,7 @@
     out_specs = (rows_spec, rows_spec, rows_spec)
 
     def device_step(hidden, cache_lat, cache_rope, seq_lens, attn_norm, w_query, w_kv_down, kv_norm, w_key_up, w_val_up, w_out, mlp_norm, w_gate, w_up, w_down):
-        resid, lat_new, rope_new = attention_block(hidden, cache_lat, cache_rope, seq_lens, attn_norm, w_query, w_kv_down, kv_norm, w_key_up, w_val_up, w_out)
-        mlp_in = rms_norm(resid, mlp_norm)
+        resid, mlp_in, lat_new, rope_new = attention_block(hidden, cache_lat, cache_rope, seq_lens, attn_norm, w_query, w_kv_down, kv_norm, w_key_up, w_val_up, w_out, mlp_norm)
         out_hidden = mlp_block(mlp_in, resid, w_gate.T, w_up.T, w_down)
         return out_hidden, lat_new, rope_new
 

time: 123 us -> 93.9 us (0.76)
  matrix products: 51.5 us -> 0 us
  Pallas kernels: 59.5 us -> 85.9 us
  other arithmetic: 7.64 us -> 0 us
  local copies, waits for them, and re-layouts: 3.35 us -> 6.86 us
    dot_general x10 -> x0, matrix products: 51.5 us -> none  [the longest x1 14.6 us: attention_block(): jnp.einsum('bhk,bsk->bhs', q_lat, cache_lat, preferred_element_type=jnp.f...]
    pallas_call x0 -> x1, Pallas kernels: none -> 26.9 us  [attention_block(): pl.pallas_call(attn_kernel, out_shape=(jax.ShapeDtypeStruct((rows, width)...]
    broadcast_in_dim x0 -> x4, local copies, waits for them, and re-layouts: none -> 5.19 us  [the longest x1 1.35 us: attention_block(): seq_lens[:, None]]
    convert_element_type x9 -> x0, other arithmetic: 3.86 us -> none  [the longest x4 2.9 us: rms_norm(): return (vals32 * inv_rms * gain.astype(jnp.float32)).astype(jnp.bfloat16)]
    reduce_sum x3 -> x0, other arithmetic: 1.8 us -> none  [the longest x2 1.21 us: rms_norm(): inv_rms = lax.rsqrt(jnp.mean(vals32 * vals32, axis=-1, keepdims=True) + EPS)]
    unnamed x13 -> x1, local copies, waits for them, and re-layouts: 2.63 us -> 1.67 us
where the time goes in v2:
time: 93.9 us; the launch traced here: 93.4 us
  Pallas kernels  85.9 us (91%)
  local copies, waits for them, and re-layouts  6.86 us (7%)
    pallas_call x1, Pallas kernels, mlp_block(): pl.pallas_call(mlp_kernel, out_shape=jax.ShapeDtypeStruct((rows, width),...  59 us
    pallas_call x1, Pallas kernels, attention_block(): pl.pallas_call(attn_kernel, out_shape=(jax.ShapeDtypeStruct((rows, width)...  26.9 us

profile of v2, /device:TPU:0, one launch (start us, length us, event | category | flops | bytes accessed | tf_op | source)
XLA Modules:
  0.0 93.4 jit_solution(180951899787885856)
XLA Ops:
  0.6 1.3 %broadcast_in_dim.14.kv_gain = bf16[1,512]{1,0:T(2,128)(2,1)} reshape(bf16[512]{0:T(512)(128)(2,1)} %param.22) | data formatting | bytes 2048 | tf_op jit(solution)/shard_map/broadcast_in_dim | solution.py:256
  1.9 1.3 %broadcast_in_dim.13.attn_gain = bf16[1,2048]{1,0:T(2,128)(2,1)} reshape(bf16[2048]{0:T(1024)(128)(2,1)} %param.19) | data formatting | bytes 8192 | tf_op jit(solution)/shard_map/broadcast_in_dim | solution.py:256
  3.2 1.3 %broadcast_in_dim.15.mlp_gain = bf16[1,2048]{1,0:T(2,128)(2,1)} reshape(bf16[2048]{0:T(1024)(128)(2,1)} %param.26) | data formatting | bytes 8192 | tf_op jit(solution)/shard_map/broadcast_in_dim | solution.py:256
  4.5 1.3 %copy.18.lens_col = s32[64,1]{1,0:T(8,128)} copy(s32[64,1]{0,1:T(1,128)} %bitcast.7) | data formatting | bytes 512 | tf_op jit(solution)/shard_map/broadcast_in_dim | solution.py:256
  5.8 26.9 %latent_attention.1 = (bf16[64,2048]{1,0:T(8,128)(2,1)}, bf16[64,2048]{1,0:T(8,128)(2,1)}, bf16[64,512]{1,0:T(8,128)(2,1)}, bf16[64,64]{1,0:T(8,128)(2,1)}) custom-call(s32[64]{0:T(128)} %lens_ref.1, bf16[64,2048]{1,0:T(8,128)(2,1)} %hidden_ref.1, s32[64,1]{1,0:T(8,128)} %copy.18.lens_col, bf16[1,2048]{1,0:T(2,128)(2,1)} %broadcast_in_dim.13.attn_gain, ...), custom_call_target="tpu_custom_call" | custom-call | flops 2902458368 | bytes 65273856 | tf_op jit(solution)/shard_map/latent_attention/pallas_call | solution.py:225
  32.7 59.0 %mlp_exchange.1 = bf16[64,2048]{1,0:T(8,128)(2,1)} custom-call(bf16[64,2048]{1,0:T(8,128)(2,1)} %get-tuple-element.7.g_ref, bf16[64,2048]{1,0:T(8,128)(2,1)} %get-tuple-element.8.resid_ref, bf16[1368,2048]{1,0:T(8,128)(2,1)} %bitcast.8, bf16[1368,2048]{1,0:T(8,128)(2,1)} %bitcast.9, bf16[1368,2048]{1,0:T(8,128)(2,1)} %wd_hbm.1), custom_call_target="tpu_custom_call" | custom-call | flops 8606711808 | bytes 16809984 | tf_op jit(solution)/shard_map/mlp_exchange/pallas_call | solution.py:501
  91.7 1.7 %copy.20 = bf16[64,2048]{1,0:T(8,128)(2,1)} copy(bf16[64,2048]{1,0:T(8,128)(2,1)} %mlp_exchange.1) | data formatting | bytes 524288

commit v3 on v2

--- a/solution.py
+++ b/solution.py
@@ -22,9 +22,9 @@
 VMEM_LIMIT = 63 * 1024 * 1024
 
 
-def attn_kernel(lens_ref, hidden_ref, lens_col, attn_gain, kv_gain, mlp_gain, lat_hbm, rope_hbm, wq_hbm, wkv_hbm, wk_hbm, wv_hbm, wo_hbm,
+def attn_kernel(lens_ref, hidden_ref, lens_vec, attn_gain, kv_gain, mlp_gain, lat_hbm, rope_hbm, wq_hbm, wkv_hbm, wk_hbm, wv_hbm, wo_hbm,
                 resid_ref, mlp_in_ref, lat_new_ref, rope_new_ref,
-                keys, rope, wq, wkv, wk, wv, wo, normed, qs, qr, lat_row, rope_row, heads_out, order, key_sem, w_sem):
+                keys, rope, wq, wkv, wk, wv, wo, normed, qs, ol, qr, lat_row, rope_row, heads_out, order, key_sem, w_sem):
     f32, bf16 = jnp.float32, jnp.bfloat16
     rows, width = hidden_ref.shape
     rank = wk.shape[0]
@@ -36,10 +36,10 @@
     w_copies = [pltpu.make_async_copy(wkv_hbm, wkv, w_sem.at[0]), pltpu.make_async_copy(wk_hbm, wk, w_sem.at[1])]
     w_copies += [pltpu.make_async_copy(wq_hbm.at[:, pl.ds(j * chunk, chunk)], wq.at[j], w_sem.at[2 + j]) for j in range(Q_CHUNKS)]
     rope_copy = pltpu.make_async_copy(rope_hbm, rope, w_sem.at[2 + Q_CHUNKS])
-    late_copies = [pltpu.make_async_copy(wv_hbm, wv, w_sem.at[3 + Q_CHUNKS]), pltpu.make_async_copy(wo_hbm, wo, w_sem.at[4 + Q_CHUNKS])]
-    for copy in w_copies:
+    late_copies = [pltpu.make_async_copy(wv_hbm, wv, w_sem.at[3 + Q_CHUNKS])]
+    late_copies += [pltpu.make_async_copy(wo_hbm.at[:, pl.ds(n * 512, 512)], wo.at[n], w_sem.at[4 + Q_CHUNKS + n]) for n in range(width // 512)]
+    for copy in w_copies[:4]:
         copy.start()
-    rope_copy.start()
 
     def kind(b):
         return lax.div(lens_ref[b], BLOCK)
@@ -89,16 +89,17 @@
         start_group(g)
         return carry
 
-    lax.fori_loop(0, SLOTS, start_first, 0)
-
     vals = hidden_ref[...].astype(f32)
     inv_rms = lax.rsqrt(jnp.mean(vals * vals, axis=-1, keepdims=True) + EPS)
-    normed[...] = (vals * inv_rms * attn_gain[...].astype(f32)).astype(bf16)
+    normed[...] = (vals * inv_rms * attn_gain[...].astype(f32)[None]).astype(bf16)
 
     lane = lax.broadcasted_iota(jnp.int32, (rows, 2 * ROPE_DIM), 1)
     half = ROPE_DIM // 2
     freq = jnp.exp(lax.rem(lane, half).astype(f32) * (-math.log(ROPE_BASE) / half))
-    angles = lens_col[...].astype(f32) * freq
+    square_ids = (rows, rows)
+    diagonal = lax.broadcasted_iota(jnp.int32, square_ids, 0) == lax.broadcasted_iota(jnp.int32, square_ids, 1)
+    lens = jnp.sum(jnp.where(diagonal, lens_vec[...].astype(f32)[None], 0.0), axis=1, keepdims=True)
+    angles = lens * freq
     cos_tab = jnp.cos(angles)
     is_first = lax.rem(lane, ROPE_DIM) < half
     sin_tab = jnp.where(is_first, -jnp.sin(angles), jnp.sin(angles))
@@ -108,10 +109,12 @@
         return (pair * cos_tab + swapped * sin_tab).astype(bf16).astype(f32)
 
     w_copies[0].wait()
+    for copy in w_copies[4:]:
+        copy.start()
     kv = lax.dot_general(normed[...], wkv[...], (((1,), (1,)), ((), ())), preferred_element_type=f32).astype(bf16).astype(f32)
     lat = kv[:, :rank]
     inv_lat = lax.rsqrt(jnp.mean(lat * lat, axis=-1, keepdims=True) + EPS)
-    lat_new = (lat * inv_lat * kv_gain[...].astype(f32)).astype(bf16)
+    lat_new = (lat * inv_lat * kv_gain[...].astype(f32)[None]).astype(bf16)
     lat_new_ref[...] = lat_new
     lat_row[...] = lat_new.astype(f32)
     pe = kv[:, rank:]
@@ -131,6 +134,10 @@
 
     for j in range(Q_CHUNKS):
         w_copies[2 + j].wait()
+        if j == 1:
+            rope_copy.start()
+        first, last = j * SLOTS // Q_CHUNKS, (j + 1) * SLOTS // Q_CHUNKS
+        lax.fori_loop(first, last, start_first, 0)
         query = jnp.dot(normed[...], wq[j], preferred_element_type=f32).astype(bf16).astype(f32)
         for pair in range(chunk // 384):
             base = pair * 384
@@ -172,10 +179,9 @@
             expo = jnp.exp(score - jnp.max(score, axis=1, keepdims=True))
             probs.append((expo / jnp.sum(expo, axis=1, keepdims=True)).astype(bf16))
         for i, b in enumerate(picks):
-            mine = pl.ds(pl.multiple_of(b * heads, heads), heads)
             out = jnp.dot(probs[i], keys[slot, i, :span], preferred_element_type=f32)
             for part in range(rank // 128):
-                qs[part, mine, :] = out[:, part * 128:(part + 1) * 128]
+                ol[part, pl.ds(b, heads, stride=rows), :] = out[:, part * 128:(part + 1) * 128]
 
     def one_group(g, carry):
         per_class(g, lambda blocks: attend(g, blocks))
@@ -184,7 +190,7 @@
         def _():
             start_group(g + SLOTS)
 
-        @pl.when(g == groups - SLOTS - 1)
+        @pl.when(g == groups - SLOTS - 2)
         def _():
             for copy in late_copies:
                 copy.start()
@@ -196,18 +202,18 @@
     late_copies[0].wait()
     for head in range(heads):
         cols = slice(head * VAL_DIM, (head + 1) * VAL_DIM)
-        lat_out = jnp.concatenate([qs[part, pl.ds(head, rows, stride=heads), :] for part in range(rank // 128)], axis=1).astype(bf16)
+        lat_out = jnp.concatenate([ol[part, head * rows:(head + 1) * rows, :] for part in range(rank // 128)], axis=1).astype(bf16)
         heads_out[:, cols] = jnp.dot(lat_out, wv[:, cols], preferred_element_type=f32).astype(bf16)
-    late_copies[1].wait()
     square = jnp.zeros((rows, 1), f32)
     for n in range(width // 512):
         cols = slice(n * 512, (n + 1) * 512)
-        attn_out = jnp.dot(heads_out[...], wo[:, cols], preferred_element_type=f32)
+        late_copies[1 + n].wait()
+        attn_out = jnp.dot(heads_out[...], wo[n], preferred_element_type=f32)
         resid = (hidden_ref[:, cols].astype(f32) + attn_out).astype(bf16)
         resid_ref[:, cols] = resid
         square = square + jnp.sum(resid.astype(f32) * resid.astype(f32), axis=-1, keepdims=True)
     inv_rms = lax.rsqrt(square * (1.0 / width) + EPS)
-    mlp_in_ref[...] = (resid_ref[...].astype(f32) * inv_rms * mlp_gain[...].astype(f32)).astype(bf16)
+    mlp_in_ref[...] = (resid_ref[...].astype(f32) * inv_rms * mlp_gain[...].astype(f32)[None]).astype(bf16)
 
 
 def attention_block(hidden, cache_lat, cache_rope, seq_lens, attn_norm, w_query, w_kv_down, kv_norm, w_key_up, w_val_up, w_out, mlp_norm):
@@ -239,8 +245,9 @@
             pltpu.VMEM((rank + ROPE_DIM, width), bf16),
             pltpu.VMEM((rank, heads * NOPE_DIM), bf16),
             pltpu.VMEM((rank, heads * VAL_DIM), bf16),
-            pltpu.VMEM((heads * VAL_DIM, width), bf16),
+            pltpu.VMEM((width // 512, heads * VAL_DIM, 512), bf16),
             pltpu.VMEM((rows, width), bf16),
+            pltpu.VMEM((rank // 128, rows * heads, 128), f32),
             pltpu.VMEM((rank // 128, rows * heads, 128), f32),
             pltpu.VMEM((rows * heads, 2 * ROPE_DIM), f32),
             pltpu.VMEM((rows, rank), f32),
@@ -248,18 +255,19 @@
             pltpu.VMEM((rows, heads * VAL_DIM), bf16),
             pltpu.SMEM((rows,), jnp.int32),
             dma((SLOTS, GROUP)),
-            dma((5 + Q_CHUNKS,)),
+            dma((4 + Q_CHUNKS + width // 512,)),
         ],
         compiler_params=pltpu.CompilerParams(vmem_limit_bytes=VMEM_LIMIT),
         cost_estimate=pl.CostEstimate(flops=flops, bytes_accessed=moved, transcendentals=rows * heads * slots),
         name='latent_attention',
-    )(seq_lens, hidden, seq_lens[:, None], attn_norm[None], kv_norm[None], mlp_norm[None], cache_lat, jnp.swapaxes(cache_rope, 1, 2), w_query, w_kv_down.T, w_key_up, w_val_up, w_out)
+    )(seq_lens, hidden, seq_lens, attn_norm, kv_norm, mlp_norm, cache_lat, jnp.swapaxes(cache_rope, 1, 2), w_query, w_kv_down.T, w_key_up, w_val_up, w_out)
 
 
 MESH = pl.DeviceIdType.MESH
 NSUB = 2
-NRS = 4
+NRS = 8
 STRIP = 256
+HALVES = 2
 
 
 def mlp_kernel(g_ref, resid_ref, wg_hbm, wu_hbm, wd_hbm, out_ref,
@@ -287,8 +295,9 @@
     w_copies = []
     for idx, (src, dst) in enumerate(((wg_hbm, wg), (wu_hbm, wu), (wd_hbm, wd))):
         copy = pltpu.make_async_copy(src, dst, w_sem.at[idx])
-        copy.start()
         w_copies.append(copy)
+    w_copies[0].start()
+    w_copies[1].start()
 
     barrier = pltpu.get_barrier_semaphore()
     pl.semaphore_signal(barrier, inc=1, device_id={'tp': partner}, device_id_type=MESH)
@@ -337,8 +346,13 @@
         for k in range(NSUB):
             ag_d2d(landed(chip, k), chip, k).wait_recv()
 
-    def rd_copy(chip):
-        return remote(psend.at[chip], precv.at[chip], rd_send.at[chip], rd_recv.at[chip], partner)
+    def rd_copy(chip, part):
+        span = pl.ds(pl.multiple_of(part * (width // HALVES), width // HALVES), width // HALVES)
+        return remote(psend.at[chip, :, span], precv.at[chip, :, span], rd_send.at[chip, part], rd_recv.at[chip, part], partner)
+
+    def rd_wait(chip):
+        for part in range(HALVES):
+            rd_copy(chip, part).wait_recv()
 
     def rs_copy(chip, k, dst, recv_sem, dev):
         span = pl.ds(k * rsub, rsub)
@@ -349,7 +363,7 @@
         return pown[chip, span] + precv[chip, span].astype(jnp.float32)
 
     def end_send(chip):
-        rd_copy(chip).wait_recv()
+        rd_wait(chip)
         for k in range(NRS):
             rsend[chip, pl.ds(k * rsub, rsub)] = rs_base(chip, k).astype(jnp.bfloat16)
             rs_copy(chip, k, rrecv_e, rs_recv_e, dev_m).start()
@@ -362,14 +376,14 @@
             arrive(mir(3), 1, ag_send_m, dev_m)
             arrive(mir(1), 1, ag_send_e, dev_e)
 
-        at(is_int, 0, 2, int_a)
-        at(is_int, 1, 2, lambda: arrive(mir(0), 0, ag_send_e, dev_e))
-        at(is_int, 2, 1, lambda: arrive(mir(0), 1, ag_send_e, dev_e))
-        at(is_end, 0, 2, lambda: arrive(mir(2), 0, None, None))
-        at(is_end, 1, 2, lambda: arrive(mir(1), 0, None, None))
-        at(is_end, 2, 0, lambda: end_send(mir(2)))
-        at(is_end, 2, 2, lambda: arrive(mir(0), 0, None, None))
-        at(is_end, 3, 0, lambda: end_send(mir(1)))
+        at(is_int, 0, 1, int_a)
+        at(is_int, 1, 0, lambda: arrive(mir(0), 0, ag_send_e, dev_e))
+        at(is_int, 1, 3, lambda: arrive(mir(0), 1, ag_send_e, dev_e))
+        at(is_end, 0, 2, lambda: arrive(mir(1), 0, None, None))
+        at(is_end, 1, 0, lambda: end_send(mir(2)))
+        at(is_end, 1, 2, lambda: arrive(mir(0), 0, None, None))
+        at(is_end, 2, 0, lambda: end_send(mir(1)))
+        at(is_end, 3, 0, lambda: end_send(mir(0)))
 
     def swiglu(lhs, at, count):
         gate = lax.dot_general(lhs, wg[pl.ds(at, count)], (((1,), (1,)), ((), ())), preferred_element_type=jnp.float32)
@@ -380,19 +394,23 @@
     rest = ffn - whole * STRIP
 
     def one_step(step, carry):
-        third = jnp.where(is_end, mir(1), mir(1))
-        chip = jnp.where(step == 0, z, jnp.where(step == 1, jnp.where(is_end, mir(2), mir(3)), jnp.where(step == 2, third, mir(0))))
+        chip = mir(jnp.where(is_end, lax.rem(6 - step, 4), jnp.where(step == 0, 2, jnp.where(step == 1, 3, 3 - step))))
 
         @pl.when(jnp.logical_and(step == 0, is_int))
         def _():
             arrive(mir(3), 0, ag_send_m, dev_m)
             arrive(mir(1), 0, ag_send_e, dev_e)
 
+        @pl.when(jnp.logical_and(step == 0, is_end))
+        def _():
+            arrive(mir(2), 0, None, None)
+            arrive(mir(2), 1, None, None)
+
+        @pl.when(jnp.logical_and(step == 1, is_end))
+        def _():
+            arrive(mir(1), 1, None, None)
+
         @pl.when(jnp.logical_and(step == 2, is_end))
-        def _():
-            arrive(mir(1), 1, None, None)
-
-        @pl.when(jnp.logical_and(step == 3, is_end))
         def _():
             arrive(mir(0), 1, None, None)
 
@@ -402,6 +420,7 @@
         def _():
             w_copies[0].wait()
             w_copies[1].wait()
+            w_copies[2].start()
 
         def one_strip(strip, carry):
             at = pl.multiple_of(strip * STRIP, STRIP)
@@ -412,31 +431,27 @@
         lax.fori_loop(0, whole, one_strip, 0)
         act[:, whole * STRIP:] = swiglu(g_all[chip].reshape(2 * rows, width), whole * STRIP, rest)
 
-        @pl.when(jnp.logical_and(step == 0, is_end))
-        def _():
-            arrive(mir(2), 1, None, None)
-
         @pl.when(step == 0)
         def _():
             w_copies[2].wait()
 
-        def one_col(col, carry):
-            span = pl.ds(pl.multiple_of(col * STRIP, STRIP), STRIP)
-            part = jnp.dot(act[...], wd[:, span], preferred_element_type=jnp.float32)
-            pown[chip, :, span] = part[:rows]
-            psend[chip, :, span] = part[rows:].astype(jnp.bfloat16)
+        def one_part(part, carry):
+            wide = width // HALVES
+            span = pl.ds(pl.multiple_of(part * wide, wide), wide)
+            down = jnp.dot(act[...], wd[:, span], preferred_element_type=jnp.float32)
+            psend[chip, :, span] = down[rows:].astype(jnp.bfloat16)
+            pown[chip, :, span] = down[:rows]
+            rd_copy(chip, part).start()
             return carry
 
-        lax.fori_loop(0, width // STRIP, one_col, 0)
-        rd_copy(chip).start()
+        lax.fori_loop(0, HALVES, one_part, 0)
         return carry
 
     lax.fori_loop(0, 4, one_step, 0)
 
     @pl.when(is_end)
     def _():
-        end_send(mir(0))
-        rd_copy(z).wait_recv()
+        rd_wait(z)
         base = pown[z] + precv[z].astype(jnp.float32) + resid_ref[...].astype(jnp.float32)
         pown[z] = base
         for k in range(NRS):
@@ -447,7 +462,7 @@
     @pl.when(is_int)
     def _():
         def pass_on(chip, dst_in, sem_in, dst_out, sem_out, dev):
-            rd_copy(chip).wait_recv()
+            rd_wait(chip)
             for k in range(NRS):
                 span = pl.ds(k * rsub, rsub)
                 rs_copy(chip, k, dst_in, sem_in, dev_m).wait_recv()
@@ -458,7 +473,7 @@
             pass_on(chip, rrecv_e, rs_recv_e, rrecv_m, rs_recv_m, dev_m)
 
         own_send(mir(1))
-        rd_copy(z).wait_recv()
+        rd_wait(z)
         for k in range(NRS):
             rs_copy(z, k, rrecv_e, rs_recv_e, dev_m).wait_recv()
         pown[z] = pown[z] + precv[z].astype(jnp.float32) + resid_ref[...].astype(jnp.float32) + rrecv_e[z].astype(jnp.float32)
@@ -482,7 +497,8 @@
             ag_copy(landed(mir(0), k), mir(0), k, ag_send_e, dev_e).wait_send()
 
     for chip in range(4):
-        rd_copy(chip).wait_send()
+        for part in range(HALVES):
+            rd_copy(chip, part).wait_send()
 
         @pl.when(chip != z)
         def _():
@@ -517,7 +533,7 @@
             pltpu.VMEM((4, rows, width), bf16),
             dma((3,)),
             dma((4, NSUB)), dma((4, NSUB)), dma((4, NSUB)), dma((4, NSUB)), dma((4, NSUB)),
-            dma((4,)), dma((4,)),
+            dma((4, HALVES)), dma((4, HALVES)),
             dma((4, NRS)), dma((4, NRS)), dma((4, NRS)),
         ],
         compiler_params=pltpu.CompilerParams(collective_id=0, has_side_effects=True, vmem_limit_bytes=60 * 1024 * 1024),

time: 93.9 us -> 85 us (0.905)
  local copies, waits for them, and re-layouts: 6.86 us -> 1.67 us
  Pallas kernels: 85.9 us -> 82.4 us
    pallas_call x1, Pallas kernels: 59 us -> 53.8 us  [mlp_block(): pl.pallas_call(mlp_kernel, out_shape=jax.ShapeDtypeStruct((rows, width),...]
    broadcast_in_dim x4 -> x0, local copies, waits for them, and re-layouts: 5.19 us -> none  [the longest x1 1.35 us: attention_block(): seq_lens[:, None]]
    pallas_call x1, Pallas kernels: 26.9 us -> 28.6 us  [attention_block(): pl.pallas_call(attn_kernel, out_shape=(jax.ShapeDtypeStruct((rows, width)...]
where the time goes in v3:
time: 85 us; the launch traced here: 84.7 us
  Pallas kernels  82.4 us (97%)
  local copies, waits for them, and re-layouts  1.67 us (2%)
    pallas_call x1, Pallas kernels, mlp_block(): pl.pallas_call(mlp_kernel, out_shape=jax.ShapeDtypeStruct((rows, width),...  53.8 us
    pallas_call x1, Pallas kernels, attention_block(): pl.pallas_call(attn_kernel, out_shape=(jax.ShapeDtypeStruct((rows, width)...  28.6 us

profile of v3, /device:TPU:0, one launch (start us, length us, event | category | flops | bytes accessed | tf_op | source)
XLA Modules:
  0.0 84.7 jit_solution(12985805341799350072)
XLA Ops:
  0.6 28.6 %latent_attention.1 = (bf16[64,2048]{1,0:T(8,128)(2,1)}, bf16[64,2048]{1,0:T(8,128)(2,1)}, bf16[64,512]{1,0:T(8,128)(2,1)}, bf16[64,64]{1,0:T(8,128)(2,1)}) custom-call(s32[64]{0:T(128)} %lens_vec.1, bf16[64,2048]{1,0:T(8,128)(2,1)} %hidden_ref.1, s32[64]{0:T(128)} %lens_vec.1, bf16[2048]{0:T(1024)(128)(2,1)} %attn_gain.1, bf16[512]{0:T(512)(128)(2,1)} %kv_gain.1, ...), custom_call_target="tpu_custom_call" | custom-call | flops 2902458368 | bytes 65273856 | tf_op jit(solution)/shard_map/latent_attention/pallas_call | solution.py:231
  29.3 53.8 %mlp_exchange.1 = bf16[64,2048]{1,0:T(8,128)(2,1)} custom-call(bf16[64,2048]{1,0:T(8,128)(2,1)} %get-tuple-element.7.g_ref, bf16[64,2048]{1,0:T(8,128)(2,1)} %get-tuple-element.8.resid_ref, bf16[1368,2048]{1,0:T(8,128)(2,1)} %bitcast.6, bf16[1368,2048]{1,0:T(8,128)(2,1)} %bitcast.7, bf16[1368,2048]{1,0:T(8,128)(2,1)} %wd_hbm.1), custom_call_target="tpu_custom_call" | custom-call | flops 8606711808 | bytes 16809984 | tf_op jit(solution)/shard_map/mlp_exchange/pallas_call | solution.py:517
  83.0 1.7 %copy.19 = bf16[64,2048]{1,0:T(8,128)(2,1)} copy(bf16[64,2048]{1,0:T(8,128)(2,1)} %mlp_exchange.1) | data formatting | bytes 524288

commit v4 on v3

--- a/solution.py
+++ b/solution.py
@@ -38,8 +38,9 @@
     rope_copy = pltpu.make_async_copy(rope_hbm, rope, w_sem.at[2 + Q_CHUNKS])
     late_copies = [pltpu.make_async_copy(wv_hbm, wv, w_sem.at[3 + Q_CHUNKS])]
     late_copies += [pltpu.make_async_copy(wo_hbm.at[:, pl.ds(n * 512, 512)], wo.at[n], w_sem.at[4 + Q_CHUNKS + n]) for n in range(width // 512)]
-    for copy in w_copies[:4]:
+    for copy in w_copies:
         copy.start()
+    rope_copy.start()
 
     def kind(b):
         return lax.div(lens_ref[b], BLOCK)
@@ -88,6 +89,8 @@
     def start_first(g, carry):
         start_group(g)
         return carry
+
+    lax.fori_loop(0, SLOTS, start_first, 0)
 
     vals = hidden_ref[...].astype(f32)
     inv_rms = lax.rsqrt(jnp.mean(vals * vals, axis=-1, keepdims=True) + EPS)
@@ -109,8 +112,6 @@
         return (pair * cos_tab + swapped * sin_tab).astype(bf16).astype(f32)
 
     w_copies[0].wait()
-    for copy in w_copies[4:]:
-        copy.start()
     kv = lax.dot_general(normed[...], wkv[...], (((1,), (1,)), ((), ())), preferred_element_type=f32).astype(bf16).astype(f32)
     lat = kv[:, :rank]
     inv_lat = lax.rsqrt(jnp.mean(lat * lat, axis=-1, keepdims=True) + EPS)
@@ -134,10 +135,6 @@
 
     for j in range(Q_CHUNKS):
         w_copies[2 + j].wait()
-        if j == 1:
-            rope_copy.start()
-        first, last = j * SLOTS // Q_CHUNKS, (j + 1) * SLOTS // Q_CHUNKS
-        lax.fori_loop(first, last, start_first, 0)
         query = jnp.dot(normed[...], wq[j], preferred_element_type=f32).astype(bf16).astype(f32)
         for pair in range(chunk // 384):
             base = pair * 384
@@ -266,15 +263,17 @@
 MESH = pl.DeviceIdType.MESH
 NSUB = 2
 NRS = 8
-STRIP = 256
+STRIP = 512
 HALVES = 2
+TURN = 128
 
 
 def mlp_kernel(g_ref, resid_ref, wg_hbm, wu_hbm, wd_hbm, out_ref,
-               g_all, wg, wu, wd, act, pown, psend, precv, rsend, rrecv_e, rrecv_m,
-               w_sem, ag_recv, ag_recv_d, ag_send_e, ag_send_m, ag_send_d,
+               g_all, wg_rows, wu_rows, wg, wu, wd, act, pown, psend, precv, rsend, rrecv_e, rrecv_m,
+               w_sem, d_sem, ag_recv, ag_recv_d, ag_send_e, ag_send_m, ag_send_d,
                rd_recv, rd_send, rs_recv_e, rs_recv_m, rs_send):
-    ffn = wg.shape[0]
+    ffn = wd.shape[0]
+    padded = wg.shape[1]
     rows, width = g_ref.shape
     sub = rows // NSUB
     rsub = rows // NRS
@@ -292,12 +291,26 @@
     dev_e = jnp.where(is_end, me, 2 * mir(3) + c)
     dev_m = 2 * jnp.where(is_end, mir(2), mir(1)) + c
 
-    w_copies = []
-    for idx, (src, dst) in enumerate(((wg_hbm, wg), (wu_hbm, wu), (wd_hbm, wd))):
-        copy = pltpu.make_async_copy(src, dst, w_sem.at[idx])
-        w_copies.append(copy)
-    w_copies[0].start()
-    w_copies[1].start()
+    turns = padded // TURN
+    last = ffn - (turns - 1) * TURN
+
+    def w_piece(src, dst, idx, at, count):
+        return pltpu.make_async_copy(src.at[pl.ds(at * TURN, count)], dst.at[pl.ds(at * TURN, count)], w_sem.at[idx, at])
+
+    def w_both(at, count):
+        return [w_piece(wg_hbm, wg_rows, 0, at, count), w_piece(wu_hbm, wu_rows, 1, at, count)]
+
+    down_copy = pltpu.make_async_copy(wd_hbm, wd, d_sem)
+
+    def start_piece(at, carry):
+        for copy in w_both(at, TURN):
+            copy.start()
+        return carry
+
+    lax.fori_loop(0, turns - 1, start_piece, 0)
+    for copy in w_both(turns - 1, last):
+        copy.start()
+    down_copy.start()
 
     barrier = pltpu.get_barrier_semaphore()
     pl.semaphore_signal(barrier, inc=1, device_id={'tp': partner}, device_id_type=MESH)
@@ -370,42 +383,55 @@
 
     def hook(step, strip):
         def at(role, want_step, want_strip, fn):
-            pl.when(jnp.logical_and(role, jnp.logical_and(step == want_step, strip == want_strip)))(fn)
-
-        def int_a():
-            arrive(mir(3), 1, ag_send_m, dev_m)
-            arrive(mir(1), 1, ag_send_e, dev_e)
-
-        at(is_int, 0, 1, int_a)
-        at(is_int, 1, 0, lambda: arrive(mir(0), 0, ag_send_e, dev_e))
-        at(is_int, 1, 3, lambda: arrive(mir(0), 1, ag_send_e, dev_e))
-        at(is_end, 0, 2, lambda: arrive(mir(1), 0, None, None))
+            if strip == want_strip:
+                pl.when(jnp.logical_and(role, step == want_step))(fn)
+
+        at(is_int, 0, 1, lambda: arrive(mir(0), 0, ag_send_e, dev_e))
+        at(is_int, 1, 0, lambda: arrive(mir(0), 1, ag_send_e, dev_e))
+        at(is_end, 0, 0, lambda: arrive(mir(1), 0, None, None))
         at(is_end, 1, 0, lambda: end_send(mir(2)))
-        at(is_end, 1, 2, lambda: arrive(mir(0), 0, None, None))
+        at(is_end, 1, 1, lambda: arrive(mir(0), 0, None, None))
         at(is_end, 2, 0, lambda: end_send(mir(1)))
         at(is_end, 3, 0, lambda: end_send(mir(0)))
 
-    def swiglu(lhs, at, count):
-        gate = lax.dot_general(lhs, wg[pl.ds(at, count)], (((1,), (1,)), ((), ())), preferred_element_type=jnp.float32)
-        up = lax.dot_general(lhs, wu[pl.ds(at, count)], (((1,), (1,)), ((), ())), preferred_element_type=jnp.float32)
+    def swiglu(lhs, span):
+        gate = jnp.dot(lhs, wg[:, span], preferred_element_type=jnp.float32)
+        up = jnp.dot(lhs, wu[:, span], preferred_element_type=jnp.float32)
         return (gate / (1.0 + jnp.exp(-gate)) * up).astype(jnp.bfloat16)
 
-    whole = ffn // STRIP
-    rest = ffn - whole * STRIP
+    def first_arrivals(k):
+        @pl.when(is_int)
+        def _():
+            arrive(mir(3), k, ag_send_m, dev_m)
+            arrive(mir(1), k, ag_send_e, dev_e)
+
+        @pl.when(is_end)
+        def _():
+            arrive(mir(2), k, None, None)
+
+    def turn(at, carry):
+        span = pl.ds(pl.multiple_of(at * TURN, TURN), TURN)
+        for copy in w_both(at, TURN):
+            copy.wait()
+        wg[:, span] = wg_rows[span].T
+        wu[:, span] = wu_rows[span].T
+        pl.when(at == turns // 2)(lambda: first_arrivals(0))
+        return carry
+
+    lax.fori_loop(0, turns - 1, turn, 0)
+    for copy in w_both(turns - 1, last):
+        copy.wait()
+    tail = slice((turns - 1) * TURN, padded)
+    for src in (wg_rows, wu_rows):
+        src[ffn:] = jnp.zeros((padded - ffn, width), jnp.bfloat16)
+    wg[:, tail] = wg_rows[tail].T
+    wu[:, tail] = wu_rows[tail].T
+    first_arrivals(1)
+
 
     def one_step(step, carry):
         chip = mir(jnp.where(is_end, lax.rem(6 - step, 4), jnp.where(step == 0, 2, jnp.where(step == 1, 3, 3 - step))))
 
-        @pl.when(jnp.logical_and(step == 0, is_int))
-        def _():
-            arrive(mir(3), 0, ag_send_m, dev_m)
-            arrive(mir(1), 0, ag_send_e, dev_e)
-
-        @pl.when(jnp.logical_and(step == 0, is_end))
-        def _():
-            arrive(mir(2), 0, None, None)
-            arrive(mir(2), 1, None, None)
-
         @pl.when(jnp.logical_and(step == 1, is_end))
         def _():
             arrive(mir(1), 1, None, None)
@@ -416,29 +442,19 @@
 
         both(chip)
 
+        for strip, at in enumerate(range(0, padded, STRIP)):
+            span = slice(at, min(at + STRIP, padded))
+            act[:, span] = swiglu(g_all[chip].reshape(2 * rows, width), span)
+            hook(step, strip)
+
         @pl.when(step == 0)
         def _():
-            w_copies[0].wait()
-            w_copies[1].wait()
-            w_copies[2].start()
-
-        def one_strip(strip, carry):
-            at = pl.multiple_of(strip * STRIP, STRIP)
-            act[:, pl.ds(at, STRIP)] = swiglu(g_all[chip].reshape(2 * rows, width), at, STRIP)
-            hook(step, strip)
-            return carry
-
-        lax.fori_loop(0, whole, one_strip, 0)
-        act[:, whole * STRIP:] = swiglu(g_all[chip].reshape(2 * rows, width), whole * STRIP, rest)
-
-        @pl.when(step == 0)
-        def _():
-            w_copies[2].wait()
+            down_copy.wait()
 
         def one_part(part, carry):
             wide = width // HALVES
             span = pl.ds(pl.multiple_of(part * wide, wide), wide)
-            down = jnp.dot(act[...], wd[:, span], preferred_element_type=jnp.float32)
+            down = jnp.dot(act[:, :ffn], wd[:, span], preferred_element_type=jnp.float32)
             psend[chip, :, span] = down[rows:].astype(jnp.bfloat16)
             pown[chip, :, span] = down[:rows]
             rd_copy(chip, part).start()
@@ -509,6 +525,7 @@
 def mlp_block(mlp_in, resid, w_gate_t, w_up_t, w_down):
     rows, width = mlp_in.shape
     ffn = w_gate_t.shape[0]
+    padded = -(-ffn // TURN) * TURN
     bf16, f32 = jnp.bfloat16, jnp.float32
     vmem = pl.BlockSpec(memory_space=pltpu.VMEM)
     hbm = pl.BlockSpec(memory_space=pl.ANY)
@@ -521,17 +538,20 @@
         out_specs=vmem,
         scratch_shapes=[
             pltpu.VMEM((4, 2, rows, width), bf16),
+            pltpu.VMEM((padded, width), bf16),
+            pltpu.VMEM((padded, width), bf16),
+            pltpu.VMEM((width, padded), bf16),
+            pltpu.VMEM((width, padded), bf16),
             pltpu.VMEM((ffn, width), bf16),
-            pltpu.VMEM((ffn, width), bf16),
-            pltpu.VMEM((ffn, width), bf16),
-            pltpu.VMEM((2 * rows, ffn), bf16),
+            pltpu.VMEM((2 * rows, padded), bf16),
             pltpu.VMEM((4, rows, width), f32),
             pltpu.VMEM((4, rows, width), bf16),
             pltpu.VMEM((4, rows, width), bf16),
             pltpu.VMEM((4, rows, width), bf16),
             pltpu.VMEM((4, rows, width), bf16),
             pltpu.VMEM((4, rows, width), bf16),
-            dma((3,)),
+            dma((2, padded // TURN)),
+            dma,
             dma((4, NSUB)), dma((4, NSUB)), dma((4, NSUB)), dma((4, NSUB)), dma((4, NSUB)),
             dma((4, HALVES)), dma((4, HALVES)),
             dma((4, NRS)), dma((4, NRS)), dma((4, NRS)),

time: 85 us -> 79.4 us (0.934)
  Pallas kernels: 82.4 us -> 76.6 us
    pallas_call x1, Pallas kernels: 53.8 us -> 48 us  [mlp_block(): pl.pallas_call(mlp_kernel, out_shape=jax.ShapeDtypeStruct((rows, width),...]
where the time goes in v4:
time: 79.4 us; the launch traced here: 78.9 us
  Pallas kernels  76.6 us (96%)
  local copies, waits for them, and re-layouts  1.67 us (2%)
    pallas_call x1, Pallas kernels, mlp_block(): pl.pallas_call(mlp_kernel, out_shape=jax.ShapeDtypeStruct((rows, width),...  48 us
    pallas_call x1, Pallas kernels, attention_block(): pl.pallas_call(attn_kernel, out_shape=(jax.ShapeDtypeStruct((rows, width)...  28.6 us
    unnamed x1, local copies, waits for them, and re-layouts  1.67 us

profile of v4, /device:TPU:0, one launch (start us, length us, event | category | flops | bytes accessed | tf_op | source)
XLA Modules:
  0.0 78.9 jit_solution(9703290557582379138)
XLA Ops:
  0.6 28.6 %latent_attention.1 = (bf16[64,2048]{1,0:T(8,128)(2,1)}, bf16[64,2048]{1,0:T(8,128)(2,1)}, bf16[64,512]{1,0:T(8,128)(2,1)}, bf16[64,64]{1,0:T(8,128)(2,1)}) custom-call(s32[64]{0:T(128)} %lens_vec.1, bf16[64,2048]{1,0:T(8,128)(2,1)} %hidden_ref.1, s32[64]{0:T(128)} %lens_vec.1, bf16[2048]{0:T(1024)(128)(2,1)} %attn_gain.1, bf16[512]{0:T(512)(128)(2,1)} %kv_gain.1, ...), custom_call_target="tpu_custom_call" | custom-call | flops 2902458368 | bytes 65273856 | tf_op jit(solution)/shard_map/latent_attention/pallas_call | solution.py:228
  29.2 48.0 %mlp_exchange.1 = bf16[64,2048]{1,0:T(8,128)(2,1)} custom-call(bf16[64,2048]{1,0:T(8,128)(2,1)} %get-tuple-element.7.g_ref, bf16[64,2048]{1,0:T(8,128)(2,1)} %get-tuple-element.8.resid_ref, bf16[1368,2048]{1,0:T(8,128)(2,1)} %bitcast.6, bf16[1368,2048]{1,0:T(8,128)(2,1)} %bitcast.7, bf16[1368,2048]{1,0:T(8,128)(2,1)} %wd_hbm.1), custom_call_target="tpu_custom_call" | custom-call | flops 8606711808 | bytes 16809984 | tf_op jit(solution)/shard_map/mlp_exchange/pallas_call | solution.py:534
  77.2 1.7 %copy.19 = bf16[64,2048]{1,0:T(8,128)(2,1)} copy(bf16[64,2048]{1,0:T(8,128)(2,1)} %mlp_exchange.1) | data formatting | bytes 524288

commit v5 on v4

--- a/solution.py
+++ b/solution.py
@@ -15,8 +15,10 @@
 SCALE = (NOPE_DIM + ROPE_DIM) ** -0.5
 
 
-GROUP = 4
-SLOTS = 7
+GROUP = 8
+SLOTS = 4
+LAG = 2
+PITCH = 72
 BLOCK = 128
 Q_CHUNKS = 4
 VMEM_LIMIT = 63 * 1024 * 1024
@@ -151,7 +153,6 @@
         span = blocks * BLOCK
         for copy in group_copies(g, blocks):
             copy.wait()
-        scores = []
         picks = [order[g * GROUP + i] for i in range(GROUP)]
         for i, b in enumerate(picks):
             length = lens_ref[b]
@@ -159,7 +160,9 @@
             tile = keys[slot, i, pl.ds(base, 16), :].astype(f32)
             sub = lax.broadcasted_iota(jnp.int32, (16, rank), 0)
             keys[slot, i, pl.ds(base, 16), :] = jnp.where(sub == length - base, lat_row[pl.ds(b, 1), :], tile).astype(bf16)
-        for i, b in enumerate(picks):
+
+        def score_of(i):
+            b = picks[i]
             length = lens_ref[b]
             mine = pl.ds(pl.multiple_of(b * heads, heads), heads)
             q_lat = jnp.concatenate([qs[part, mine, :] for part in range(rank // 128)], axis=1).astype(bf16)
@@ -170,15 +173,21 @@
             new = jnp.sum(jnp.where(first, q_rot * rope_row[pl.ds(b, 1), :], 0.0), axis=1, keepdims=True)
             at = lax.broadcasted_iota(jnp.int32, (heads, span), 1)
             score = (score + jnp.where(at == length, new, near)) * SCALE
-            scores.append(jnp.where(at <= length, score, -jnp.inf))
-        probs = []
-        for score in scores:
+            return jnp.where(at <= length, score, -jnp.inf)
+
+        def finish(i, score):
             expo = jnp.exp(score - jnp.max(score, axis=1, keepdims=True))
-            probs.append((expo / jnp.sum(expo, axis=1, keepdims=True)).astype(bf16))
-        for i, b in enumerate(picks):
-            out = jnp.dot(probs[i], keys[slot, i, :span], preferred_element_type=f32)
+            prob = (expo / jnp.sum(expo, axis=1, keepdims=True)).astype(bf16)
+            out = jnp.dot(prob, keys[slot, i, :span], preferred_element_type=f32)
             for part in range(rank // 128):
-                ol[part, pl.ds(b, heads, stride=rows), :] = out[:, part * 128:(part + 1) * 128]
+                ol[part, pl.ds(picks[i], heads, stride=PITCH), :] = out[:, part * 128:(part + 1) * 128]
+
+        scores = {}
+        for i in range(GROUP + LAG):
+            if i < GROUP:
+                scores[i] = score_of(i)
+            if i >= LAG:
+                finish(i - LAG, scores.pop(i - LAG))
 
     def one_group(g, carry):
         per_class(g, lambda blocks: attend(g, blocks))
@@ -187,7 +196,7 @@
         def _():
             start_group(g + SLOTS)
 
-        @pl.when(g == groups - SLOTS - 2)
+        @pl.when(g == groups - SLOTS - 1)
         def _():
             for copy in late_copies:
                 copy.start()
@@ -199,7 +208,7 @@
     late_copies[0].wait()
     for head in range(heads):
         cols = slice(head * VAL_DIM, (head + 1) * VAL_DIM)
-        lat_out = jnp.concatenate([ol[part, head * rows:(head + 1) * rows, :] for part in range(rank // 128)], axis=1).astype(bf16)
+        lat_out = jnp.concatenate([ol[part, head * PITCH:head * PITCH + rows, :] for part in range(rank // 128)], axis=1).astype(bf16)
         heads_out[:, cols] = jnp.dot(lat_out, wv[:, cols], preferred_element_type=f32).astype(bf16)
     square = jnp.zeros((rows, 1), f32)
     for n in range(width // 512):
@@ -245,7 +254,7 @@
             pltpu.VMEM((width // 512, heads * VAL_DIM, 512), bf16),
             pltpu.VMEM((rows, width), bf16),
             pltpu.VMEM((rank // 128, rows * heads, 128), f32),
-            pltpu.VMEM((rank // 128, rows * heads, 128), f32),
+            pltpu.VMEM((rank // 128, PITCH * heads, 128), f32),
             pltpu.VMEM((rows * heads, 2 * ROPE_DIM), f32),
             pltpu.VMEM((rows, rank), f32),
             pltpu.VMEM((rows, 2 * ROPE_DIM), f32),

time: 79.4 us -> 79.1 us (level)
  no operation moved by 1% of the time
where the time goes in v5:
time: 79.1 us
  Pallas kernels  76.8 us (97%)
  local copies, waits for them, and re-layouts  1.67 us (2%)
    pallas_call x1, Pallas kernels, mlp_block(): pl.pallas_call(mlp_kernel, out_shape=jax.ShapeDtypeStruct((rows, width),...  48.7 us
    pallas_call x1, Pallas kernels, attention_block(): pl.pallas_call(attn_kernel, out_shape=(jax.ShapeDtypeStruct((rows, width)...  28.1 us
    unnamed x1, local copies, waits for them, and re-layouts  1.67 us

profile of v5, /device:TPU:0, one launch (start us, length us, event | category | flops | bytes accessed | tf_op | source)
XLA Modules:
  0.0 79.1 jit_solution(189632816614253519)
XLA Ops:
  0.6 28.1 %latent_attention.1 = (bf16[64,2048]{1,0:T(8,128)(2,1)}, bf16[64,2048]{1,0:T(8,128)(2,1)}, bf16[64,512]{1,0:T(8,128)(2,1)}, bf16[64,64]{1,0:T(8,128)(2,1)}) custom-call(s32[64]{0:T(128)} %lens_vec.1, bf16[64,2048]{1,0:T(8,128)(2,1)} %hidden_ref.1, s32[64]{0:T(128)} %lens_vec.1, bf16[2048]{0:T(1024)(128)(2,1)} %attn_gain.1, bf16[512]{0:T(512)(128)(2,1)} %kv_gain.1, ...), custom_call_target="tpu_custom_call" | custom-call | flops 2902458368 | bytes 65273856 | tf_op jit(solution)/shard_map/latent_attention/pallas_call | solution.py:237
  28.8 48.7 %mlp_exchange.1 = bf16[64,2048]{1,0:T(8,128)(2,1)} custom-call(bf16[64,2048]{1,0:T(8,128)(2,1)} %get-tuple-element.7.g_ref, bf16[64,2048]{1,0:T(8,128)(2,1)} %get-tuple-element.8.resid_ref, bf16[1368,2048]{1,0:T(8,128)(2,1)} %bitcast.6, bf16[1368,2048]{1,0:T(8,128)(2,1)} %bitcast.7, bf16[1368,2048]{1,0:T(8,128)(2,1)} %wd_hbm.1), custom_call_target="tpu_custom_call" | custom-call | flops 8606711808 | bytes 16809984 | tf_op jit(solution)/shard_map/mlp_exchange/pallas_call | solution.py:543
  77.4 1.7 %copy.19 = bf16[64,2048]{1,0:T(8,128)(2,1)} copy(bf16[64,2048]{1,0:T(8,128)(2,1)} %mlp_exchange.1) | data formatting | bytes 524288

commit v6 on v5

--- a/solution.py
+++ b/solution.py
@@ -167,7 +167,10 @@
             mine = pl.ds(pl.multiple_of(b * heads, heads), heads)
             q_lat = jnp.concatenate([qs[part, mine, :] for part in range(rank // 128)], axis=1).astype(bf16)
             q_rot = qr[mine, :]
-            score = lax.dot_general(q_lat, keys[slot, i, :span], (((1,), (1,)), ((), ())), preferred_element_type=f32)
+            if i % 2:
+                score = lax.dot_general(keys[slot, i, :span], q_lat, (((1,), (1,)), ((), ())), preferred_element_type=f32).T
+            else:
+                score = lax.dot_general(q_lat, keys[slot, i, :span], (((1,), (1,)), ((), ())), preferred_element_type=f32)
             near = jnp.dot(q_rot[:, :ROPE_DIM].astype(bf16), rope[b, :, :span], preferred_element_type=f32)
             first = lax.broadcasted_iota(jnp.int32, (heads, 2 * ROPE_DIM), 1) < ROPE_DIM
             new = jnp.sum(jnp.where(first, q_rot * rope_row[pl.ds(b, 1), :], 0.0), axis=1, keepdims=True)
@@ -177,7 +180,7 @@
 
         def finish(i, score):
             expo = jnp.exp(score - jnp.max(score, axis=1, keepdims=True))
-            prob = (expo / jnp.sum(expo, axis=1, keepdims=True)).astype(bf16)
+            prob = (expo * (1.0 / jnp.sum(expo, axis=1, keepdims=True))).astype(bf16)
             out = jnp.dot(prob, keys[slot, i, :span], preferred_element_type=f32)
             for part in range(rank // 128):
                 ol[part, pl.ds(picks[i], heads, stride=PITCH), :] = out[:, part * 128:(part + 1) * 128]

time: 79.1 us -> 80.3 us (1.015)
  Pallas kernels: 76.8 us -> 77.8 us
where the time goes in v6:
time: 80.3 us; the launch traced here: 80.1 us
  Pallas kernels  77.8 us (97%)
  local copies, waits for them, and re-layouts  1.67 us (2%)
    pallas_call x1, Pallas kernels, mlp_block(): pl.pallas_call(mlp_kernel, out_shape=jax.ShapeDtypeStruct((rows, width),...  48.9 us
    pallas_call x1, Pallas kernels, attention_block(): pl.pallas_call(attn_kernel, out_shape=(jax.ShapeDtypeStruct((rows, width)...  28.8 us
    unnamed x1, local copies, waits for them, and re-layouts  1.67 us

profile of v6, /device:TPU:0, one launch (start us, length us, event | category | flops | bytes accessed | tf_op | source)
XLA Modules:
  0.0 80.1 jit_solution(15826787950691880409)
XLA Ops:
  0.6 28.8 %latent_attention.1 = (bf16[64,2048]{1,0:T(8,128)(2,1)}, bf16[64,2048]{1,0:T(8,128)(2,1)}, bf16[64,512]{1,0:T(8,128)(2,1)}, bf16[64,64]{1,0:T(8,128)(2,1)}) custom-call(s32[64]{0:T(128)} %lens_vec.1, bf16[64,2048]{1,0:T(8,128)(2,1)} %hidden_ref.1, s32[64]{0:T(128)} %lens_vec.1, bf16[2048]{0:T(1024)(128)(2,1)} %attn_gain.1, bf16[512]{0:T(512)(128)(2,1)} %kv_gain.1, ...), custom_call_target="tpu_custom_call" | custom-call | flops 2902458368 | bytes 65273856 | tf_op jit(solution)/shard_map/latent_attention/pallas_call | solution.py:240
  29.5 48.9 %mlp_exchange.1 = bf16[64,2048]{1,0:T(8,128)(2,1)} custom-call(bf16[64,2048]{1,0:T(8,128)(2,1)} %get-tuple-element.7.g_ref, bf16[64,2048]{1,0:T(8,128)(2,1)} %get-tuple-element.8.resid_ref, bf16[1368,2048]{1,0:T(8,128)(2,1)} %bitcast.6, bf16[1368,2048]{1,0:T(8,128)(2,1)} %bitcast.7, bf16[1368,2048]{1,0:T(8,128)(2,1)} %wd_hbm.1), custom_call_target="tpu_custom_call" | custom-call | flops 8606711808 | bytes 16809984 | tf_op jit(solution)/shard_map/mlp_exchange/pallas_call | solution.py:546
  78.4 1.7 %copy.19 = bf16[64,2048]{1,0:T(8,128)(2,1)} copy(bf16[64,2048]{1,0:T(8,128)(2,1)} %mlp_exchange.1) | data formatting | bytes 524288

commit v7 on v4

--- a/solution.py
+++ b/solution.py
@@ -17,16 +17,19 @@
 
 GROUP = 4
 SLOTS = 7
-BLOCK = 128
+BLOCK = 64
+PITCH = 24
 Q_CHUNKS = 4
 VMEM_LIMIT = 63 * 1024 * 1024
 
 
-def attn_kernel(lens_ref, hidden_ref, lens_vec, attn_gain, kv_gain, mlp_gain, lat_hbm, rope_hbm, wq_hbm, wkv_hbm, wk_hbm, wv_hbm, wo_hbm,
+def attn_kernel(lens_ref, hidden_hbm, lens_vec, attn_gain, kv_gain, mlp_gain, lat_hbm, rope_hbm, wq_hbm, wkv_hbm, wk_hbm, wv_hbm, wo_hbm,
                 resid_ref, mlp_in_ref, lat_new_ref, rope_new_ref,
-                keys, rope, wq, wkv, wk, wv, wo, normed, qs, ol, qr, lat_row, rope_row, heads_out, order, key_sem, w_sem):
+                hidden_ref, keys, rope, wq, wkv, wk, wv, wo, normed, qs, ol, qr, lat_row, rope_row, heads_out, order, place, key_sem, w_sem, hidden_sem):
     f32, bf16 = jnp.float32, jnp.bfloat16
     rows, width = hidden_ref.shape
+    hidden_copy = pltpu.make_async_copy(hidden_hbm, hidden_ref, hidden_sem)
+    hidden_copy.start()
     rank = wk.shape[0]
     heads = wk.shape[1] // NOPE_DIM
     groups = rows // GROUP
@@ -45,28 +48,28 @@
     def kind(b):
         return lax.div(lens_ref[b], BLOCK)
 
-    def count(b, counts):
+    for i in range(classes):
+        place[i] = 0
+
+    def count(b, carry):
+        place[kind(b)] += 1
+        return carry
+
+    lax.fori_loop(0, rows, count, 0)
+    total = jnp.int32(0)
+    for i in reversed(range(classes)):
+        here = place[i]
+        place[i] = total
+        total = total + here
+
+    def put(b, carry):
         k = kind(b)
-        return tuple(n + jnp.where(k == i, 1, 0) for i, n in enumerate(counts))
-
-    zero = jnp.int32(0)
-    counts = lax.fori_loop(0, rows, count, (zero,) * classes)
-    firsts = []
-    total = zero
-    for i in reversed(range(classes)):
-        firsts.append(total)
-        total = total + counts[i]
-    firsts = tuple(reversed(firsts))
-
-    def place(b, firsts):
-        k = kind(b)
-        at = firsts[0]
-        for i in range(1, classes):
-            at = jnp.where(k == i, firsts[i], at)
+        at = place[k]
         order[at] = b
-        return tuple(n + jnp.where(k == i, 1, 0) for i, n in enumerate(firsts))
-
-    lax.fori_loop(0, rows, place, firsts)
+        place[k] = at + 1
+        return carry
+
+    lax.fori_loop(0, rows, put, 0)
 
     def group_copies(g, blocks):
         slot = lax.rem(g, SLOTS)
@@ -92,6 +95,7 @@
 
     lax.fori_loop(0, SLOTS, start_first, 0)
 
+    hidden_copy.wait()
     vals = hidden_ref[...].astype(f32)
     inv_rms = lax.rsqrt(jnp.mean(vals * vals, axis=-1, keepdims=True) + EPS)
     normed[...] = (vals * inv_rms * attn_gain[...].astype(f32)[None]).astype(bf16)
@@ -130,8 +134,8 @@
         key_up = wk[:, head * NOPE_DIM:(head + 1) * NOPE_DIM]
         q_lat = lax.dot_general(nope.astype(bf16), key_up, (((1,), (1,)), ((), ())), preferred_element_type=f32).astype(bf16).astype(f32)
         for part in range(rank // 128):
-            qs[part, pl.ds(head, rows, stride=heads), :] = q_lat[:, part * 128:(part + 1) * 128]
-        qr[pl.ds(head, rows, stride=heads), :] = pe_rot
+            qs[part, pl.ds(head, rows, stride=PITCH), :] = q_lat[:, part * 128:(part + 1) * 128]
+        qr[pl.ds(head, rows, stride=PITCH), :] = pe_rot
 
     for j in range(Q_CHUNKS):
         w_copies[2 + j].wait()
@@ -161,7 +165,7 @@
             keys[slot, i, pl.ds(base, 16), :] = jnp.where(sub == length - base, lat_row[pl.ds(b, 1), :], tile).astype(bf16)
         for i, b in enumerate(picks):
             length = lens_ref[b]
-            mine = pl.ds(pl.multiple_of(b * heads, heads), heads)
+            mine = pl.ds(pl.multiple_of(b * PITCH, 8), heads)
             q_lat = jnp.concatenate([qs[part, mine, :] for part in range(rank // 128)], axis=1).astype(bf16)
             q_rot = qr[mine, :]
             score = lax.dot_general(q_lat, keys[slot, i, :span], (((1,), (1,)), ((), ())), preferred_element_type=f32)
@@ -174,11 +178,11 @@
         probs = []
         for score in scores:
             expo = jnp.exp(score - jnp.max(score, axis=1, keepdims=True))
-            probs.append((expo / jnp.sum(expo, axis=1, keepdims=True)).astype(bf16))
+            probs.append((expo * (1.0 / jnp.sum(expo, axis=1, keepdims=True))).astype(bf16))
         for i, b in enumerate(picks):
             out = jnp.dot(probs[i], keys[slot, i, :span], preferred_element_type=f32)
             for part in range(rank // 128):
-                ol[part, pl.ds(b, heads, stride=rows), :] = out[:, part * 128:(part + 1) * 128]
+                ol[part, pl.ds(pl.multiple_of(b * PITCH, 8), heads), :] = out[:, part * 128:(part + 1) * 128]
 
     def one_group(g, carry):
         per_class(g, lambda blocks: attend(g, blocks))
@@ -199,7 +203,7 @@
     late_copies[0].wait()
     for head in range(heads):
         cols = slice(head * VAL_DIM, (head + 1) * VAL_DIM)
-        lat_out = jnp.concatenate([ol[part, head * rows:(head + 1) * rows, :] for part in range(rank // 128)], axis=1).astype(bf16)
+        lat_out = jnp.concatenate([ol[part, pl.ds(head, rows, stride=PITCH), :] for part in range(rank // 128)], axis=1).astype(bf16)
         heads_out[:, cols] = jnp.dot(lat_out, wv[:, cols], preferred_element_type=f32).astype(bf16)
     square = jnp.zeros((rows, 1), f32)
     for n in range(width // 512):
@@ -233,9 +237,10 @@
             jax.ShapeDtypeStruct((rows, rank), bf16),
             jax.ShapeDtypeStruct((rows, ROPE_DIM), bf16),
         ),
-        in_specs=[smem] + [vmem] * 5 + [hbm] * 7,
+        in_specs=[smem, hbm] + [vmem] * 4 + [hbm] * 7,
         out_specs=(vmem,) * 4,
         scratch_shapes=[
+            pltpu.VMEM((rows, width), bf16),
             pltpu.VMEM((SLOTS, GROUP, slots, rank), bf16),
             pltpu.VMEM((rows, ROPE_DIM, slots), bf16),
             pltpu.VMEM((Q_CHUNKS, width, q_width // Q_CHUNKS), bf16),
@@ -244,15 +249,17 @@
             pltpu.VMEM((rank, heads * VAL_DIM), bf16),
             pltpu.VMEM((width // 512, heads * VAL_DIM, 512), bf16),
             pltpu.VMEM((rows, width), bf16),
-            pltpu.VMEM((rank // 128, rows * heads, 128), f32),
-            pltpu.VMEM((rank // 128, rows * heads, 128), f32),
-            pltpu.VMEM((rows * heads, 2 * ROPE_DIM), f32),
+            pltpu.VMEM((rank // 128, rows * PITCH, 128), f32),
+            pltpu.VMEM((rank // 128, rows * PITCH, 128), f32),
+            pltpu.VMEM((rows * PITCH, 2 * ROPE_DIM), f32),
             pltpu.VMEM((rows, rank), f32),
             pltpu.VMEM((rows, 2 * ROPE_DIM), f32),
             pltpu.VMEM((rows, heads * VAL_DIM), bf16),
             pltpu.SMEM((rows,), jnp.int32),
+            pltpu.SMEM((slots // BLOCK,), jnp.int32),
             dma((SLOTS, GROUP)),
             dma((4 + Q_CHUNKS + width // 512,)),
+            dma,
         ],
         compiler_params=pltpu.CompilerParams(vmem_limit_bytes=VMEM_LIMIT),
         cost_estimate=pl.CostEstimate(flops=flops, bytes_accessed=moved, transcendentals=rows * heads * slots),
@@ -268,13 +275,15 @@
 TURN = 128
 
 
-def mlp_kernel(g_ref, resid_ref, wg_hbm, wu_hbm, wd_hbm, out_ref,
-               g_all, wg_rows, wu_rows, wg, wu, wd, act, pown, psend, precv, rsend, rrecv_e, rrecv_m,
-               w_sem, d_sem, ag_recv, ag_recv_d, ag_send_e, ag_send_m, ag_send_d,
+def mlp_kernel(g_hbm, resid_ref, wg_hbm, wu_hbm, wd_hbm, out_ref,
+               g_ref, g_all, wg_rows, wu_rows, wg, wu, wd, act, pown, psend, precv, rsend, rrecv_e, rrecv_m,
+               g_sem, w_sem, d_sem, ag_recv, ag_recv_d, ag_send_e, ag_send_m, ag_send_d,
                rd_recv, rd_send, rs_recv_e, rs_recv_m, rs_send):
     ffn = wd.shape[0]
     padded = wg.shape[1]
     rows, width = g_ref.shape
+    g_copy = pltpu.make_async_copy(g_hbm, g_ref, g_sem)
+    g_copy.start()
     sub = rows // NSUB
     rsub = rows // NRS
     me = lax.axis_index('tp')
@@ -334,6 +343,7 @@
     def ag_d2d(src, chip, k):
         return remote(src, g_all.at[chip, 1, pl.ds(k * sub, sub)], ag_send_d.at[chip, k], ag_recv_d.at[chip, k], partner)
 
+    g_copy.wait()
     for k in range(NSUB):
         piece = g_ref.at[pl.ds(k * sub, sub)]
         ag_copy(piece, z, k, ag_send_m, dev_m).start()
@@ -534,9 +544,10 @@
     return pl.pallas_call(
         mlp_kernel,
         out_shape=jax.ShapeDtypeStruct((rows, width), bf16),
-        in_specs=[vmem, vmem, hbm, hbm, hbm],
+        in_specs=[hbm, vmem, hbm, hbm, hbm],
         out_specs=vmem,
         scratch_shapes=[
+            pltpu.VMEM((rows, width), bf16),
             pltpu.VMEM((4, 2, rows, width), bf16),
             pltpu.VMEM((padded, width), bf16),
             pltpu.VMEM((padded, width), bf16),
@@ -550,6 +561,7 @@
             pltpu.VMEM((4, rows, width), bf16),
             pltpu.VMEM((4, rows, width), bf16),
             pltpu.VMEM((4, rows, width), bf16),
+            dma,
             dma((2, padded // TURN)),
             dma,
             dma((4, NSUB)), dma((4, NSUB)), dma((4, NSUB)), dma((4, NSUB)), dma((4, NSUB)),

time: 79.4 us -> 81.4 us (1.025)
  Pallas kernels: 76.6 us -> 78.9 us
    pallas_call x1, Pallas kernels: 28.6 us -> 30.9 us  [attention_block(): pl.pallas_call(attn_kernel, out_shape=(jax.ShapeDtypeStruct((rows, width)...]
where the time goes in v7:
time: 81.4 us; the launch traced here: 81.3 us
  Pallas kernels  78.9 us (97%)
  local copies, waits for them, and re-layouts  1.67 us (2%)
    pallas_call x1, Pallas kernels, mlp_block(): pl.pallas_call(mlp_kernel, out_shape=jax.ShapeDtypeStruct((rows, width),...  48 us
    pallas_call x1, Pallas kernels, attention_block(): pl.pallas_call(attn_kernel, out_shape=(jax.ShapeDtypeStruct((rows, width)...  30.9 us
    unnamed x1, local copies, waits for them, and re-layouts  1.67 us

profile of v7, /device:TPU:0, one launch (start us, length us, event | category | flops | bytes accessed | tf_op | source)
XLA Modules:
  0.0 81.3 jit_solution(18185239731682933489)
XLA Ops:
  0.6 30.9 %latent_attention.1 = (bf16[64,2048]{1,0:T(8,128)(2,1)}, bf16[64,2048]{1,0:T(8,128)(2,1)}, bf16[64,512]{1,0:T(8,128)(2,1)}, bf16[64,64]{1,0:T(8,128)(2,1)}) custom-call(s32[64]{0:T(128)} %lens_vec.1, bf16[64,2048]{1,0:T(8,128)(2,1)} %hidden_hbm.1, s32[64]{0:T(128)} %lens_vec.1, bf16[2048]{0:T(1024)(128)(2,1)} %attn_gain.1, bf16[512]{0:T(512)(128)(2,1)} %kv_gain.1, ...), custom_call_target="tpu_custom_call" | custom-call | flops 2902458368 | bytes 65273856 | tf_op jit(solution)/shard_map/latent_attention/pallas_call | solution.py:232
  31.6 48.0 %mlp_exchange.1 = bf16[64,2048]{1,0:T(8,128)(2,1)} custom-call(bf16[64,2048]{1,0:T(8,128)(2,1)} %get-tuple-element.7.g_hbm, bf16[64,2048]{1,0:T(8,128)(2,1)} %get-tuple-element.8.resid_ref, bf16[1368,2048]{1,0:T(8,128)(2,1)} %bitcast.6, bf16[1368,2048]{1,0:T(8,128)(2,1)} %bitcast.7, bf16[1368,2048]{1,0:T(8,128)(2,1)} %wd_hbm.1), custom_call_target="tpu_custom_call" | custom-call | flops 8606711808 | bytes 16809984 | tf_op jit(solution)/shard_map/mlp_exchange/pallas_call | solution.py:544
  79.6 1.7 %copy.19 = bf16[64,2048]{1,0:T(8,128)(2,1)} copy(bf16[64,2048]{1,0:T(8,128)(2,1)} %mlp_exchange.1) | data formatting | bytes 524288

commit v8 on v4

--- a/solution.py
+++ b/solution.py
@@ -24,7 +24,7 @@
 
 def attn_kernel(lens_ref, hidden_ref, lens_vec, attn_gain, kv_gain, mlp_gain, lat_hbm, rope_hbm, wq_hbm, wkv_hbm, wk_hbm, wv_hbm, wo_hbm,
                 resid_ref, mlp_in_ref, lat_new_ref, rope_new_ref,
-                keys, rope, wq, wkv, wk, wv, wo, normed, qs, ol, qr, lat_row, rope_row, heads_out, order, key_sem, w_sem):
+                keys, rope, wq, wkv, wk, wv, wo, normed, qs, qr, lat_row, rope_row, heads_out, order, key_sem, w_sem):
     f32, bf16 = jnp.float32, jnp.bfloat16
     rows, width = hidden_ref.shape
     rank = wk.shape[0]
@@ -176,9 +176,10 @@
             expo = jnp.exp(score - jnp.max(score, axis=1, keepdims=True))
             probs.append((expo / jnp.sum(expo, axis=1, keepdims=True)).astype(bf16))
         for i, b in enumerate(picks):
+            mine = pl.ds(pl.multiple_of(b * heads, heads), heads)
             out = jnp.dot(probs[i], keys[slot, i, :span], preferred_element_type=f32)
             for part in range(rank // 128):
-                ol[part, pl.ds(b, heads, stride=rows), :] = out[:, part * 128:(part + 1) * 128]
+                qs[part, mine, :] = out[:, part * 128:(part + 1) * 128]
 
     def one_group(g, carry):
         per_class(g, lambda blocks: attend(g, blocks))
@@ -199,7 +200,7 @@
     late_copies[0].wait()
     for head in range(heads):
         cols = slice(head * VAL_DIM, (head + 1) * VAL_DIM)
-        lat_out = jnp.concatenate([ol[part, head * rows:(head + 1) * rows, :] for part in range(rank // 128)], axis=1).astype(bf16)
+        lat_out = jnp.concatenate([qs[part, pl.ds(head, rows, stride=heads), :] for part in range(rank // 128)], axis=1).astype(bf16)
         heads_out[:, cols] = jnp.dot(lat_out, wv[:, cols], preferred_element_type=f32).astype(bf16)
     square = jnp.zeros((rows, 1), f32)
     for n in range(width // 512):
@@ -244,7 +245,6 @@
             pltpu.VMEM((rank, heads * VAL_DIM), bf16),
             pltpu.VMEM((width // 512, heads * VAL_DIM, 512), bf16),
             pltpu.VMEM((rows, width), bf16),
-            pltpu.VMEM((rank // 128, rows * heads, 128), f32),
             pltpu.VMEM((rank // 128, rows * heads, 128), f32),
             pltpu.VMEM((rows * heads, 2 * ROPE_DIM), f32),
             pltpu.VMEM((rows, rank), f32),

time: 79.4 us -> 78.5 us (0.989)
  no operation moved by 1% of the time
where the time goes in v8:
time: 78.5 us; the launch traced here: 78.3 us
  Pallas kernels  76 us (97%)
  local copies, waits for them, and re-layouts  1.67 us (2%)
    pallas_call x1, Pallas kernels, mlp_block(): pl.pallas_call(mlp_kernel, out_shape=jax.ShapeDtypeStruct((rows, width),...  48.1 us
    pallas_call x1, Pallas kernels, attention_block(): pl.pallas_call(attn_kernel, out_shape=(jax.ShapeDtypeStruct((rows, width)...  27.9 us
    unnamed x1, local copies, waits for them, and re-layouts  1.67 us

profile of v8, /device:TPU:0, one launch (start us, length us, event | category | flops | bytes accessed | tf_op | source)
XLA Modules:
  0.0 78.3 jit_solution(9581464522388131017)
XLA Ops:
  0.6 27.9 %latent_attention.1 = (bf16[64,2048]{1,0:T(8,128)(2,1)}, bf16[64,2048]{1,0:T(8,128)(2,1)}, bf16[64,512]{1,0:T(8,128)(2,1)}, bf16[64,64]{1,0:T(8,128)(2,1)}) custom-call(s32[64]{0:T(128)} %lens_vec.1, bf16[64,2048]{1,0:T(8,128)(2,1)} %hidden_ref.1, s32[64]{0:T(128)} %lens_vec.1, bf16[2048]{0:T(1024)(128)(2,1)} %attn_gain.1, bf16[512]{0:T(512)(128)(2,1)} %kv_gain.1, ...), custom_call_target="tpu_custom_call" | custom-call | flops 2902458368 | bytes 65273856 | tf_op jit(solution)/shard_map/latent_attention/pallas_call | solution.py:229
  28.5 48.1 %mlp_exchange.1 = bf16[64,2048]{1,0:T(8,128)(2,1)} custom-call(bf16[64,2048]{1,0:T(8,128)(2,1)} %get-tuple-element.7.g_ref, bf16[64,2048]{1,0:T(8,128)(2,1)} %get-tuple-element.8.resid_ref, bf16[1368,2048]{1,0:T(8,128)(2,1)} %bitcast.6, bf16[1368,2048]{1,0:T(8,128)(2,1)} %bitcast.7, bf16[1368,2048]{1,0:T(8,128)(2,1)} %wd_hbm.1), custom_call_target="tpu_custom_call" | custom-call | flops 8606711808 | bytes 16809984 | tf_op jit(solution)/shard_map/mlp_exchange/pallas_call | solution.py:534
  76.6 1.7 %copy.19 = bf16[64,2048]{1,0:T(8,128)(2,1)} copy(bf16[64,2048]{1,0:T(8,128)(2,1)} %mlp_exchange.1) | data formatting | bytes 524288

commit v9 on v5

--- a/solution.py
+++ b/solution.py
@@ -18,7 +18,6 @@
 GROUP = 8
 SLOTS = 4
 LAG = 2
-PITCH = 72
 BLOCK = 128
 Q_CHUNKS = 4
 VMEM_LIMIT = 63 * 1024 * 1024
@@ -26,7 +25,7 @@
 
 def attn_kernel(lens_ref, hidden_ref, lens_vec, attn_gain, kv_gain, mlp_gain, lat_hbm, rope_hbm, wq_hbm, wkv_hbm, wk_hbm, wv_hbm, wo_hbm,
                 resid_ref, mlp_in_ref, lat_new_ref, rope_new_ref,
-                keys, rope, wq, wkv, wk, wv, wo, normed, qs, ol, qr, lat_row, rope_row, heads_out, order, key_sem, w_sem):
+                keys, rope, wq, wkv, wk, wv, wo, normed, qs, qr, lat_row, rope_row, heads_out, order, key_sem, w_sem):
     f32, bf16 = jnp.float32, jnp.bfloat16
     rows, width = hidden_ref.shape
     rank = wk.shape[0]
@@ -177,10 +176,11 @@
 
         def finish(i, score):
             expo = jnp.exp(score - jnp.max(score, axis=1, keepdims=True))
-            prob = (expo / jnp.sum(expo, axis=1, keepdims=True)).astype(bf16)
+            prob = (expo * (1.0 / jnp.sum(expo, axis=1, keepdims=True))).astype(bf16)
+            mine = pl.ds(pl.multiple_of(picks[i] * heads, heads), heads)
             out = jnp.dot(prob, keys[slot, i, :span], preferred_element_type=f32)
             for part in range(rank // 128):
-                ol[part, pl.ds(picks[i], heads, stride=PITCH), :] = out[:, part * 128:(part + 1) * 128]
+                qs[part, mine, :] = out[:, part * 128:(part + 1) * 128]
 
         scores = {}
         for i in range(GROUP + LAG):
@@ -208,7 +208,7 @@
     late_copies[0].wait()
     for head in range(heads):
         cols = slice(head * VAL_DIM, (head + 1) * VAL_DIM)
-        lat_out = jnp.concatenate([ol[part, head * PITCH:head * PITCH + rows, :] for part in range(rank // 128)], axis=1).astype(bf16)
+        lat_out = jnp.concatenate([qs[part, pl.ds(head, rows, stride=heads), :] for part in range(rank // 128)], axis=1).astype(bf16)
         heads_out[:, cols] = jnp.dot(lat_out, wv[:, cols], preferred_element_type=f32).astype(bf16)
     square = jnp.zeros((rows, 1), f32)
     for n in range(width // 512):
@@ -254,7 +254,6 @@
             pltpu.VMEM((width // 512, heads * VAL_DIM, 512), bf16),
             pltpu.VMEM((rows, width), bf16),
             pltpu.VMEM((rank // 128, rows * heads, 128), f32),
-            pltpu.VMEM((rank // 128, PITCH * heads, 128), f32),
             pltpu.VMEM((rows * heads, 2 * ROPE_DIM), f32),
             pltpu.VMEM((rows, rank), f32),
             pltpu.VMEM((rows, 2 * ROPE_DIM), f32),
@@ -369,7 +368,7 @@
             ag_d2d(landed(chip, k), chip, k).wait_recv()
 
     def rd_copy(chip, part):
-        span = pl.ds(pl.multiple_of(part * (width // HALVES), width // HALVES), width // HALVES)
+        span = pl.ds(part * (width // HALVES), width // HALVES)
         return remote(psend.at[chip, :, span], precv.at[chip, :, span], rd_send.at[chip, part], rd_recv.at[chip, part], partner)
 
     def rd_wait(chip):
@@ -460,16 +459,14 @@
         def _():
             down_copy.wait()
 
-        def one_part(part, carry):
+        for part in range(HALVES):
             wide = width // HALVES
-            span = pl.ds(pl.multiple_of(part * wide, wide), wide)
+            span = slice(part * wide, (part + 1) * wide)
             down = jnp.dot(act[:, :ffn], wd[:, span], preferred_element_type=jnp.float32)
             psend[chip, :, span] = down[rows:].astype(jnp.bfloat16)
             pown[chip, :, span] = down[:rows]
             rd_copy(chip, part).start()
-            return carry
-
-        lax.fori_loop(0, HALVES, one_part, 0)
+
         return carry
 
     lax.fori_loop(0, 4, one_step, 0)

time: 79.1 us -> 81.1 us (1.025)
  Pallas kernels: 76.8 us -> 78.5 us
    pallas_call x1, Pallas kernels: 28.1 us -> 30.3 us  [attention_block(): pl.pallas_call(attn_kernel, out_shape=(jax.ShapeDtypeStruct((rows, width)...]
where the time goes in v9:
time: 81.1 us; the launch traced here: 80.8 us
  Pallas kernels  78.5 us (97%)
  local copies, waits for them, and re-layouts  1.67 us (2%)
    pallas_call x1, Pallas kernels, mlp_block(): pl.pallas_call(mlp_kernel, out_shape=jax.ShapeDtypeStruct((rows, width),...  48.1 us
    pallas_call x1, Pallas kernels, attention_block(): pl.pallas_call(attn_kernel, out_shape=(jax.ShapeDtypeStruct((rows, width)...  30.3 us
    unnamed x1, local copies, waits for them, and re-layouts  1.67 us

profile of v9, /device:TPU:0, one launch (start us, length us, event | category | flops | bytes accessed | tf_op | source)
XLA Modules:
  0.0 80.8 jit_solution(754994094076621102)
XLA Ops:
  0.6 30.3 %latent_attention.1 = (bf16[64,2048]{1,0:T(8,128)(2,1)}, bf16[64,2048]{1,0:T(8,128)(2,1)}, bf16[64,512]{1,0:T(8,128)(2,1)}, bf16[64,64]{1,0:T(8,128)(2,1)}) custom-call(s32[64]{0:T(128)} %lens_vec.1, bf16[64,2048]{1,0:T(8,128)(2,1)} %hidden_ref.1, s32[64]{0:T(128)} %lens_vec.1, bf16[2048]{0:T(1024)(128)(2,1)} %attn_gain.1, bf16[512]{0:T(512)(128)(2,1)} %kv_gain.1, ...), custom_call_target="tpu_custom_call" | custom-call | flops 2902458368 | bytes 65273856 | tf_op jit(solution)/shard_map/latent_attention/pallas_call | solution.py:237
  31.0 48.1 %mlp_exchange.1 = bf16[64,2048]{1,0:T(8,128)(2,1)} custom-call(bf16[64,2048]{1,0:T(8,128)(2,1)} %get-tuple-element.7.g_ref, bf16[64,2048]{1,0:T(8,128)(2,1)} %get-tuple-element.8.resid_ref, bf16[1368,2048]{1,0:T(8,128)(2,1)} %bitcast.6, bf16[1368,2048]{1,0:T(8,128)(2,1)} %bitcast.7, bf16[1368,2048]{1,0:T(8,128)(2,1)} %wd_hbm.1), custom_call_target="tpu_custom_call" | custom-call | flops 8606711808 | bytes 16809984 | tf_op jit(solution)/shard_map/mlp_exchange/pallas_call | solution.py:540
  79.1 1.7 %copy.19 = bf16[64,2048]{1,0:T(8,128)(2,1)} copy(bf16[64,2048]{1,0:T(8,128)(2,1)} %mlp_exchange.1) | data formatting | bytes 524288

commit v10 on v9

--- a/solution.py
+++ b/solution.py
@@ -176,7 +176,7 @@
 
         def finish(i, score):
             expo = jnp.exp(score - jnp.max(score, axis=1, keepdims=True))
-            prob = (expo * (1.0 / jnp.sum(expo, axis=1, keepdims=True))).astype(bf16)
+            prob = (expo / jnp.sum(expo, axis=1, keepdims=True)).astype(bf16)
             mine = pl.ds(pl.multiple_of(picks[i] * heads, heads), heads)
             out = jnp.dot(prob, keys[slot, i, :span], preferred_element_type=f32)
             for part in range(rank // 128):

time: 81.1 us -> 81.3 us (level)
    pallas_call x1, Pallas kernels: 48.1 us -> 49.3 us  [mlp_block(): pl.pallas_call(mlp_kernel, out_shape=jax.ShapeDtypeStruct((rows, width),...]
where the time goes in v10:
time: 81.3 us; the launch traced here: 81.1 us
  Pallas kernels  78.8 us (97%)
  local copies, waits for them, and re-layouts  1.67 us (2%)
    pallas_call x1, Pallas kernels, mlp_block(): pl.pallas_call(mlp_kernel, out_shape=jax.ShapeDtypeStruct((rows, width),...  49.3 us
    pallas_call x1, Pallas kernels, attention_block(): pl.pallas_call(attn_kernel, out_shape=(jax.ShapeDtypeStruct((rows, width)...  29.5 us
    unnamed x1, local copies, waits for them, and re-layouts  1.67 us

profile of v10, /device:TPU:0, one launch (start us, length us, event | category | flops | bytes accessed | tf_op | source)
XLA Modules:
  0.0 81.1 jit_solution(754994094076621102)
XLA Ops:
  0.6 29.5 %latent_attention.1 = (bf16[64,2048]{1,0:T(8,128)(2,1)}, bf16[64,2048]{1,0:T(8,128)(2,1)}, bf16[64,512]{1,0:T(8,128)(2,1)}, bf16[64,64]{1,0:T(8,128)(2,1)}) custom-call(s32[64]{0:T(128)} %lens_vec.1, bf16[64,2048]{1,0:T(8,128)(2,1)} %hidden_ref.1, s32[64]{0:T(128)} %lens_vec.1, bf16[2048]{0:T(1024)(128)(2,1)} %attn_gain.1, bf16[512]{0:T(512)(128)(2,1)} %kv_gain.1, ...), custom_call_target="tpu_custom_call" | custom-call | flops 2902458368 | bytes 65273856 | tf_op jit(solution)/shard_map/latent_attention/pallas_call | solution.py:237
  30.2 49.3 %mlp_exchange.1 = bf16[64,2048]{1,0:T(8,128)(2,1)} custom-call(bf16[64,2048]{1,0:T(8,128)(2,1)} %get-tuple-element.7.g_ref, bf16[64,2048]{1,0:T(8,128)(2,1)} %get-tuple-element.8.resid_ref, bf16[1368,2048]{1,0:T(8,128)(2,1)} %bitcast.6, bf16[1368,2048]{1,0:T(8,128)(2,1)} %bitcast.7, bf16[1368,2048]{1,0:T(8,128)(2,1)} %wd_hbm.1), custom_call_target="tpu_custom_call" | custom-call | flops 8606711808 | bytes 16809984 | tf_op jit(solution)/shard_map/mlp_exchange/pallas_call | solution.py:540
  79.5 1.7 %copy.19 = bf16[64,2048]{1,0:T(8,128)(2,1)} copy(bf16[64,2048]{1,0:T(8,128)(2,1)} %mlp_exchange.1) | data formatting | bytes 524288
